TPU v7x, 32 devices: a whole 2x2x4 slice. The times are simulated.
32 devices in a mesh: spin: 2 (over core), band: 8 (over z, x), grid: 2 (over y).
Axes of the slice: x: 2, y: 2, z: 4, core: 2. Of those that a mesh axis runs over, the one named last changes fastest.
Arguments:
- orbitals: bfloat16 [2, 64, 128, 128, 128], P('spin', 'band', 'grid'), may hold values from -0.14941406 to 0.14941406
- partial_bands: int32 [2, 2], P('spin'), may hold values from 0 to 63
- core_density: float32 [128, 128, 128], P('grid'), may hold values from 0.002 to 0.2
Outputs:
- potential: float32 [2, 128, 128, 128], P('spin', 'grid', 'band')
Inputs may be any that keep to these rules, and one draw needn't show every extreme that they name: `partial_bands`: row s holds, for spin s, the first half-occupied band and the count of half-occupied bands; bands past 64 - 1 do not exist.
All inputs are finite; a program needn't handle non-finite values.
Results may differ from a plain program's by a relative error of at most 0.0003.
Values sent between devices are 32-bit elements; how exact they have to be, the bound alone decides.
A program may use at most 128 MiB of HBM per device.

v0:
```python
import math

import jax
import jax.numpy as jnp
from jax import lax
from jax.sharding import PartitionSpec as P

KAPPA = 0.804
MU_X = 0.2195149727645171
BETA = 0.06672455060314922
GAMMA = (1.0 - math.log(2.0)) / math.pi**2
FZ_NORM = 2.0 ** (4.0 / 3.0) - 2.0
FPP_ZERO = 1.709921
EXACT = lax.Precision.HIGHEST


def swapped(block, axis, stride):
    count = lax.axis_size(axis)
    route = []
    for low in range(count):
        high = low | 1 << stride
        if high != low and high < count:
            route += [(low, high), (high, low)]
    return lax.ppermute(block, axis, route)


def pw_fit(radius, amp, alpha, beta_one, beta_two, beta_three, beta_four):
    root = jnp.sqrt(radius)
    denom = (
        2.0
        * amp
        * (
            beta_one * root
            + beta_two * radius
            + beta_three * radius * root
            + beta_four * radius * radius
        )
    )
    return -2.0 * amp * (1.0 + alpha * radius) * jnp.log(1.0 + 1.0 / denom)


def exchange_part(double, sigma_four):
    kfermi = (3.0 * math.pi**2 * double) ** (1.0 / 3.0)
    scaled = sigma_four / (4.0 * kfermi * kfermi * double * double)
    enhance = 1.0 + KAPPA - KAPPA / (1.0 + MU_X * scaled / KAPPA)
    return -0.75 / math.pi * kfermi * double * enhance


def xc_energy(n_up, n_down, s_uu, s_ud, s_dd):
    exch = 0.5 * (exchange_part(2.0 * n_up, 4.0 * s_uu) + exchange_part(2.0 * n_down, 4.0 * s_dd))
    total = n_up + n_down
    zeta = (n_up - n_down) / total
    radius = (3.0 / (4.0 * math.pi * total)) ** (1.0 / 3.0)
    ec_para = pw_fit(radius, 0.031091, 0.2137, 7.5957, 3.5876, 1.6382, 0.49294)
    ec_ferro = pw_fit(radius, 0.015545, 0.20548, 14.1189, 6.1977, 3.3662, 0.62517)
    neg_stiff = pw_fit(radius, 0.016887, 0.11125, 10.357, 3.6231, 0.88026, 0.49671)
    plus_z = 1.0 + zeta
    minus_z = 1.0 - zeta
    fzeta = (plus_z ** (4.0 / 3.0) + minus_z ** (4.0 / 3.0) - 2.0) / FZ_NORM
    zeta_four = zeta**4
    ec_lda = (
        ec_para
        - neg_stiff * fzeta / FPP_ZERO * (1.0 - zeta_four)
        + (ec_ferro - ec_para) * fzeta * zeta_four
    )
    phi = 0.5 * (plus_z ** (2.0 / 3.0) + minus_z ** (2.0 / 3.0))
    phi_cube = phi * phi * phi
    kfermi = (3.0 * math.pi**2 * total) ** (1.0 / 3.0)
    screen_sq = 4.0 * kfermi / math.pi
    sigma = s_uu + 2.0 * s_ud + s_dd
    tsq = sigma / (4.0 * phi * phi * screen_sq * total * total)
    amp = BETA / GAMMA / (jnp.exp(-ec_lda / (GAMMA * phi_cube)) - 1.0)
    atsq = amp * tsq
    gradient_term = (
        GAMMA
        * phi_cube
        * jnp.log(1.0 + BETA / GAMMA * tsq * (1.0 + atsq) / (1.0 + atsq + atsq * atsq))
    )
    return exch + total * (ec_lda + gradient_term)


def spectral_table(length):
    index = jnp.arange(length, dtype=jnp.int32)
    phase = index[:, None] * index[None, :] % length
    angle = 2.0 * math.pi / length * phase.astype(jnp.float32)
    mode = jnp.where(index < length // 2, index, index - length)
    mode = jnp.where(index == length // 2, 0, mode)
    wave = 2.0 * math.pi / length * mode.astype(jnp.float32)
    sines = jnp.sin(angle)
    cosines = jnp.cos(angle)
    first_term = jnp.dot(sines * wave[None, :], cosines.T, precision=EXACT)
    second_term = jnp.dot(cosines * wave[None, :], sines.T, precision=EXACT)
    return (second_term - first_term) / length


def along_first(stack, table):
    return jnp.einsum("jl,flyz->fjyz", table, stack, precision=EXACT)


def along_second(stack, table):
    return jnp.einsum("jl,fxlz->fxjz", table, stack, precision=EXACT)


def along_third(stack, table):
    return jnp.einsum("fxyl,jl->fxyj", stack, table, precision=EXACT)


def pencil_axes(first, second, third, tables):
    deriv_x = lax.all_to_all(
        along_first(
            lax.all_to_all(first, "grid", split_axis=2, concat_axis=1, tiled=True), tables[0]
        ),
        "grid",
        split_axis=1,
        concat_axis=2,
        tiled=True,
    )
    deriv_y = lax.all_to_all(
        along_second(
            lax.all_to_all(second, "band", split_axis=1, concat_axis=2, tiled=True), tables[1]
        ),
        "band",
        split_axis=2,
        concat_axis=1,
        tiled=True,
    )
    return (deriv_x, deriv_y, along_third(third, tables[2]))


def per_device(orbitals, partial_bands, core_density):
    states = orbitals[0]
    count_local, x_rows, y_cols, z_cells = states.shape
    band_ids = lax.axis_index("band") * count_local + jnp.arange(count_local, dtype=jnp.int32)
    first_band = partial_bands[0, 0]
    span = partial_bands[0, 1]
    weights = jnp.where((band_ids >= first_band) & (band_ids < first_band + span), 0.5, 1.0).astype(
        jnp.float32
    )
    values = states.astype(jnp.float32)
    partial_value = jnp.sum(weights[:, None, None, None] * values * values, axis=0)
    tables = (
        spectral_table(x_rows * lax.axis_size("grid")),
        spectral_table(y_cols),
        spectral_table(z_cells),
    )
    y_block = y_cols // lax.axis_size("band")
    density = lax.psum_scatter(partial_value, "band", scatter_dimension=1, tiled=True)
    core_part = lax.dynamic_slice_in_dim(core_density, lax.axis_index("band") * y_block, y_block, 1)
    own = density + 0.5 * core_part
    single = own[None]
    steep = jnp.concatenate(pencil_axes(single, single, single, tables), axis=0)
    sent = jnp.concatenate([single, steep], axis=0)
    got = swapped(sent, "spin", 0)
    other = got[0]
    other_steep = got[1:]
    is_up = lax.axis_index("spin") == 0
    dens_up = jnp.where(is_up, own, other)
    dens_down = jnp.where(is_up, other, own)
    grad_up = jnp.where(is_up, steep, other_steep)
    grad_down = jnp.where(is_up, other_steep, steep)
    s_uu = jnp.sum(grad_up * grad_up, axis=0)
    s_ud = jnp.sum(grad_up * grad_down, axis=0)
    s_dd = jnp.sum(grad_down * grad_down, axis=0)
    energy, pull = jax.vjp(xc_energy, dens_up, dens_down, s_uu, s_ud, s_dd)
    derivs = pull(jnp.ones_like(energy))
    dn_own = jnp.where(is_up, derivs[0], derivs[1])
    ds_own = jnp.where(is_up, derivs[2], derivs[4])
    flux = 2.0 * ds_own[None] * steep + derivs[3][None] * other_steep
    div_x, div_y, div_z = pencil_axes(flux[0:1], flux[1:2], flux[2:3], tables)
    potential = dn_own - (div_x[0] + div_y[0] + div_z[0])
    return potential[None]


def solution(mesh):
    in_specs = (P("spin", "band", "grid", None, None), P("spin", None), P("grid", None, None))
    out_specs = P("spin", "grid", "band", None)
    return jax.shard_map(
        per_device, mesh=mesh, in_specs=in_specs, out_specs=out_specs, check_vma=False
    )
```

profile of v0, /device:TPU:0, one launch (start us, length us, event | category | flops | bytes accessed | tf_op | source)
XLA Modules:
  0.0 276.9 jit_solution(1300706851235047275)
XLA Ops:
  6.5 0.0 reduce-scatter.2.cloned.1.call-start
  6.5 1.3 fusion.123
  9.1 0.6 and_select_fusion
  9.8 14.0 %fusion = f32[64,128,128]{2,1,0:T(8,128)} fusion(bf16[1,8,64,128,128]{4,3,2,1,0:T(8,128)(2,1)} %param.3, f32[8]{0:T(128)S(1)} %and_select_fusion), kind=kLoop, calls=%fused_computation.1 | loop fusion | flops 32505856 | bytes 20971552 | tf_op jit(solution)/shard_map/reduce_sum | solution.py:140
  23.8 0.0 reduce-scatter.2.cloned.1.call-update
  23.8 91.5 %reduce-scatter.2.cloned.1.call-done = f32[64,16,128]{2,1,0:T(8,128)} async-done(((f32[64,128,128]{2,1,0:T(8,128)}), f32[64,16,128]{2,1,0:T(8,128)}) %reduce-scatter.2.cloned.1.call-update) | async-done | bytes 524304 | tf_op jit(solution)/shard_map/reduce_scatter | solution.py:147
  115.4 2.1 multiply_add_fusion.6
  117.4 1.2 copy.46
  118.6 10.3 %all_to_all.126 = f32[1,64,16,128]{3,1,0,2:T(8,128)S(1)} all-to-all(f32[1,64,16,128]{3,1,0,2:T(8,128)S(1)} %copy.46), channel_id=1, replica_groups=mesh['spin'=2,'band'=8,'grid'=2] {'grid'}, dimensions={2} | all-to-all | bytes 1048576 | tf_op jit(solution)/shard_map/all_to_all | solution.py:111
  129.0 4.8 %all-to-all-start.2 = ((f32[1,64,16,128]{3,2,0,1:T(8,128)}), f32[1,64,16,128]{3,2,0,1:T(8,128)S(1)}, u32[]{:S(2)}, u32[]{:S(2)}) async-start(f32[1,64,16,128]{3,2,0,1:T(8,128)} %bitcast.13), calls=%async_computation.3 | async-start | bytes 1048576 | tf_op jit(solution)/shard_map/all_to_all | solution.py:120
  133.8 0.5 fusion.95
  134.3 0.5 fusion.4
  134.8 0.3 copy.82
  135.2 1.0 convolution_bitcast_fusion.4
  136.2 1.0 copy.50
  137.2 10.3 %all-to-all-done.2 = f32[1,64,16,128]{3,2,0,1:T(8,128)S(1)} async-done(((f32[1,64,16,128]{3,2,0,1:T(8,128)}), f32[1,64,16,128]{3,2,0,1:T(8,128)S(1)}, u32[]{:S(2)}, u32[]{:S(2)}) %all-to-all-start.2) | async-done | bytes 524320 | tf_op jit(solution)/shard_map/all_to_all | solution.py:120
  147.5 3.5 %all-to-all-start.1 = ((f32[1,128,8,128]{3,2,0,1:T(8,128)}), f32[1,128,8,128]{3,2,0,1:T(8,128)S(1)}, u32[]{:S(2)}, u32[]{:S(2)}) async-start(f32[1,128,8,128]{3,2,0,1:T(8,128)} %copy.50), calls=%async_computation.2 | async-start | bytes 1048576 | tf_op jit(solution)/shard_map/all_to_all | solution.py:109
  151.0 1.0 convolution_bitcast_fusion.3
  152.1 1.0 copy.55
  153.0 4.7 %all-to-all-done.1 = f32[1,128,8,128]{3,2,0,1:T(8,128)S(1)} async-done(((f32[1,128,8,128]{3,2,0,1:T(8,128)}), f32[1,128,8,128]{3,2,0,1:T(8,128)S(1)}, u32[]{:S(2)}, u32[]{:S(2)}) %all-to-all-start.1) | async-done | bytes 524320 | tf_op jit(solution)/shard_map/all_to_all | solution.py:109
  157.8 4.4 %all-to-all-start.3 = ((f32[1,8,128,128]{3,1,0,2:T(8,128)}), f32[1,8,128,128]{3,1,0,2:T(8,128)S(1)}, u32[]{:S(2)}, u32[]{:S(2)}) async-start(f32[1,8,128,128]{3,1,0,2:T(8,128)} %copy.55), calls=%async_computation.4 | async-start | bytes 1048576 | tf_op jit(solution)/shard_map/all_to_all | solution.py:118
  162.1 1.6 convolution_bitcast_fusion.2
  163.8 11.2 %all-to-all-done.3 = f32[1,8,128,128]{3,1,0,2:T(8,128)S(1)} async-done(((f32[1,8,128,128]{3,1,0,2:T(8,128)}), f32[1,8,128,128]{3,1,0,2:T(8,128)S(1)}, u32[]{:S(2)}, u32[]{:S(2)}) %all-to-all-start.3) | async-done | bytes 524320 | tf_op jit(solution)/shard_map/all_to_all | solution.py:118
  175.0 0.1 copy.56
  175.2 2.5 pad_maximum_fusion
  177.7 0.0 collective-permute-start
  177.7 4.5 %collective-permute-done = f32[4,64,16,128]{3,2,1,0:T(8,128)} collective-permute-done((f32[4,64,16,128]{3,2,1,0:T(8,128)}, f32[4,64,16,128]{3,2,1,0:T(8,128)}, u32[]{:S(2)}, u32[]{:S(2)}) %collective-permute-start) | collective-permute-done | bytes 2097184 | tf_op jit(solution)/shard_map/ppermute | solution.py:24
  182.2 2.1 multiply_reduce_fusion.1
  184.3 0.0 copy-start
  184.3 0.0 copy-start.2
  184.3 0.0 copy-start.4
  184.3 8.5 %select_multiply_fusion = (f32[64,16,128]{2,1,0:T(8,128)S(1)}, f32[64,16,128]{2,1,0:T(8,128)S(1)}, f32[64,16,128]{2,1,0:T(8,128)}, f32[64,16,128]{2,1,0:T(8,128)}, f32[64,16,128]{2,1,0:T(8,128)}) fusion(pred[]{:T(512)S(6)} %eq.18, f32[64,16,128]{2,1,0:T(8,128)S(1)} %get-tuple-element.7, f32[64,16,128]{2,1,0:T(8,128)S(1)} %get-tuple-element.6, ...), kind=kLoop, calls=%fused_computation.101 | loop fusion | flops 21757952 | bytes 5242881 | tf_op jit(solution)/shard_map/mul | solution.py:168
  192.8 0.0 copy-done
  192.8 0.0 copy-done.2
  192.8 0.0 copy-done.4
  192.9 1.7 multiply_add_fusion
  194.6 0.9 fusion.122
  195.4 3.7 %all-to-all-start.6 = ((f32[1,64,16,128]{3,2,0,1:T(8,128)}), f32[1,64,16,128]{3,2,0,1:T(8,128)S(1)}, u32[]{:S(2)}, u32[]{:S(2)}) async-start(f32[1,64,16,128]{3,2,0,1:T(8,128)} %get-tuple-element.14), calls=%async_computation.7 | async-start | bytes 1048576 | tf_op jit(solution)/shard_map/all_to_all | solution.py:120
  199.1 1.0 copy.58
  200.1 13.8 %all-to-all-done.6 = f32[1,64,16,128]{3,2,0,1:T(8,128)S(1)} async-done(((f32[1,64,16,128]{3,2,0,1:T(8,128)}), f32[1,64,16,128]{3,2,0,1:T(8,128)S(1)}, u32[]{:S(2)}, u32[]{:S(2)}) %all-to-all-start.6) | async-done | bytes 524320 | tf_op jit(solution)/shard_map/all_to_all | solution.py:120
  213.9 3.7 %all-to-all-start.4 = ((f32[1,64,16,128]{3,1,0,2:T(8,128)}), f32[1,64,16,128]{3,1,0,2:T(8,128)S(1)}, u32[]{:S(2)}, u32[]{:S(2)}) async-start(f32[1,64,16,128]{3,1,0,2:T(8,128)} %copy.58), calls=%async_computation.5 | async-start | bytes 1048576 | tf_op jit(solution)/shard_map/all_to_all | solution.py:111
  217.7 1.0 convolution_bitcast_fusion
  218.7 1.0 copy.67
  219.7 4.9 %all-to-all-done.4 = f32[1,64,16,128]{3,1,0,2:T(8,128)S(1)} async-done(((f32[1,64,16,128]{3,1,0,2:T(8,128)}), f32[1,64,16,128]{3,1,0,2:T(8,128)S(1)}, u32[]{:S(2)}, u32[]{:S(2)}) %all-to-all-start.4) | async-done | bytes 524320 | tf_op jit(solution)/shard_map/all_to_all | solution.py:111
  224.5 4.9 %all-to-all-start.7 = ((f32[1,8,128,128]{3,1,0,2:T(8,128)}), f32[1,8,128,128]{3,1,0,2:T(8,128)S(1)}, u32[]{:S(2)}, u32[]{:S(2)}) async-start(f32[1,8,128,128]{3,1,0,2:T(8,128)} %copy.67), calls=%async_computation.8 | async-start | bytes 1048576 | tf_op jit(solution)/shard_map/all_to_all | solution.py:118
  229.5 0.3 copy.80
  229.8 1.0 convolution_bitcast_fusion.1
  230.8 1.0 copy.62
  231.8 11.5 %all-to-all-done.7 = f32[1,8,128,128]{3,1,0,2:T(8,128)S(1)} async-done(((f32[1,8,128,128]{3,1,0,2:T(8,128)}), f32[1,8,128,128]{3,1,0,2:T(8,128)S(1)}, u32[]{:S(2)}, u32[]{:S(2)}) %all-to-all-start.7) | async-done | bytes 524320 | tf_op jit(solution)/shard_map/all_to_all | solution.py:118
  243.3 3.5 %all-to-all-start.5 = ((f32[1,128,8,128]{3,2,0,1:T(8,128)}), f32[1,128,8,128]{3,2,0,1:T(8,128)S(1)}, u32[]{:S(2)}, u32[]{:S(2)}) async-start(f32[1,128,8,128]{3,2,0,1:T(8,128)} %copy.62), calls=%async_computation.6 | async-start | bytes 1048576 | tf_op jit(solution)/shard_map/all_to_all | solution.py:109
  246.8 0.1 copy.68
  246.9 0.0 copy-start.1
  247.0 6.6 %all-to-all-done.5 = f32[1,128,8,128]{3,2,0,1:T(8,128)S(1)} async-done(((f32[1,128,8,128]{3,2,0,1:T(8,128)}), f32[1,128,8,128]{3,2,0,1:T(8,128)S(1)}, u32[]{:S(2)}, u32[]{:S(2)}) %all-to-all-start.5) | async-done | bytes 524320 | tf_op jit(solution)/shard_map/all_to_all | solution.py:109
  253.6 0.0 copy-start.3
  253.6 0.0 copy-start.5
  253.6 0.0 copy-start.6
  253.6 0.1 bitcast_add_fusion
  253.6 0.0 copy-done.1
  253.7 1.0 copy-done.3
  254.6 0.2 copy-done.5
  254.8 0.2 copy-done.6
  254.9 15.2 %fusion.2 = f32[1,64,16,128]{3,2,1,0:T(8,128)} fusion(f32[64,16,128]{2,1,0:T(8,128)S(1)} %bitcast_add_fusion, f32[128,128,1]{1,0,2:T(8,128)S(1)} %fusion.4, f32[3,64,16,128]{3,2,1,0:T(8,128)S(1)} %multiply_add_fusion, f32[64,16,128]{2,1,0:T(8,128)S(1)} %copy-done.6, f32[64,16,128]{2,1,0:T(8,128)S(1)} %copy-done.3, f32[64,16,128]{2,1,0:T(8,128)S(1)} %copy-done.5, ...), kind=kOutput, calls=%fused_computation.17 | convolution fusion | flops 252182528 | bytes 4784129 | tf_op jit(solution)/shard_map/fxyl,jl->fxyj/dot_general | solution.py:105
  (9 shorter events, 0.3 us)
Async XLA Ops:
  6.5 108.8 %reduce-scatter.2.cloned.1.call-start = ((), (), s32[]{:S(2)}) async-start(), calls=%async_computation.9 | async-start | bytes 4718592 | tf_op jit(solution)/shard_map/reduce_scatter | solution.py:147
  129.0 18.6 %all-to-all-start.2 = ((f32[1,64,16,128]{3,2,0,1:T(8,128)}), f32[1,64,16,128]{3,2,0,1:T(8,128)S(1)}, u32[]{:S(2)}, u32[]{:S(2)}) async-start(f32[1,64,16,128]{3,2,0,1:T(8,128)} %bitcast.13), calls=%async_computation.3 | async-start | bytes 1048576 | tf_op jit(solution)/shard_map/all_to_all | solution.py:120
  147.5 10.3 %all-to-all-start.1 = ((f32[1,128,8,128]{3,2,0,1:T(8,128)}), f32[1,128,8,128]{3,2,0,1:T(8,128)S(1)}, u32[]{:S(2)}, u32[]{:S(2)}) async-start(f32[1,128,8,128]{3,2,0,1:T(8,128)} %copy.50), calls=%async_computation.2 | async-start | bytes 1048576 | tf_op jit(solution)/shard_map/all_to_all | solution.py:109
  157.8 17.2 %all-to-all-start.3 = ((f32[1,8,128,128]{3,1,0,2:T(8,128)}), f32[1,8,128,128]{3,1,0,2:T(8,128)S(1)}, u32[]{:S(2)}, u32[]{:S(2)}) async-start(f32[1,8,128,128]{3,1,0,2:T(8,128)} %copy.55), calls=%async_computation.4 | async-start | bytes 1048576 | tf_op jit(solution)/shard_map/all_to_all | solution.py:118
  177.7 4.5 %collective-permute-start = (f32[4,64,16,128]{3,2,1,0:T(8,128)}, f32[4,64,16,128]{3,2,1,0:T(8,128)}, u32[]{:S(2)}, u32[]{:S(2)}) collective-permute-start(f32[4,64,16,128]{3,2,1,0:T(8,128)} %pad_maximum_fusion), channel_id=1, source_target_pairs={{0,16},{16,0},{1,17},{17,1},{2,18},{18,2},{3,19},{19,3},{4,20},{20... | collective-permute-start | bytes 6291464 | tf_op jit(solution)/shard_map/ppermute | solution.py:24
  184.3 8.6 %copy-start = (f32[64,16,128]{2,1,0:T(8,128)}, f32[64,16,128]{2,1,0:T(8,128)S(1)}, u32[]{:S(2)}) copy-start(f32[64,16,128]{2,1,0:T(8,128)S(1)} %get-tuple-element.5) | copy-start | bytes 1572868
  184.3 8.6 %copy-start.2 = (f32[64,16,128]{2,1,0:T(8,128)}, f32[64,16,128]{2,1,0:T(8,128)S(1)}, u32[]{:S(2)}) copy-start(f32[64,16,128]{2,1,0:T(8,128)S(1)} %get-tuple-element.6) | copy-start | bytes 1572868
  184.3 8.6 %copy-start.4 = (f32[64,16,128]{2,1,0:T(8,128)}, f32[64,16,128]{2,1,0:T(8,128)S(1)}, u32[]{:S(2)}) copy-start(f32[64,16,128]{2,1,0:T(8,128)S(1)} %get-tuple-element.7) | copy-start | bytes 1572868
  195.4 18.5 %all-to-all-start.6 = ((f32[1,64,16,128]{3,2,0,1:T(8,128)}), f32[1,64,16,128]{3,2,0,1:T(8,128)S(1)}, u32[]{:S(2)}, u32[]{:S(2)}) async-start(f32[1,64,16,128]{3,2,0,1:T(8,128)} %get-tuple-element.14), calls=%async_computation.7 | async-start | bytes 1048576 | tf_op jit(solution)/shard_map/all_to_all | solution.py:120
  213.9 10.6 %all-to-all-start.4 = ((f32[1,64,16,128]{3,1,0,2:T(8,128)}), f32[1,64,16,128]{3,1,0,2:T(8,128)S(1)}, u32[]{:S(2)}, u32[]{:S(2)}) async-start(f32[1,64,16,128]{3,1,0,2:T(8,128)} %copy.58), calls=%async_computation.5 | async-start | bytes 1048576 | tf_op jit(solution)/shard_map/all_to_all | solution.py:111
  224.5 18.8 %all-to-all-start.7 = ((f32[1,8,128,128]{3,1,0,2:T(8,128)}), f32[1,8,128,128]{3,1,0,2:T(8,128)S(1)}, u32[]{:S(2)}, u32[]{:S(2)}) async-start(f32[1,8,128,128]{3,1,0,2:T(8,128)} %copy.67), calls=%async_computation.8 | async-start | bytes 1048576 | tf_op jit(solution)/shard_map/all_to_all | solution.py:118
  243.3 10.3 %all-to-all-start.5 = ((f32[1,128,8,128]{3,2,0,1:T(8,128)}), f32[1,128,8,128]{3,2,0,1:T(8,128)S(1)}, u32[]{:S(2)}, u32[]{:S(2)}) async-start(f32[1,128,8,128]{3,2,0,1:T(8,128)} %copy.62), calls=%async_computation.6 | async-start | bytes 1048576 | tf_op jit(solution)/shard_map/all_to_all | solution.py:109
  246.9 6.7 %copy-start.1 = (f32[64,16,128]{2,1,0:T(8,128)S(1)}, f32[64,16,128]{2,1,0:T(8,128)}, u32[]{:S(2)}) copy-start(f32[64,16,128]{2,1,0:T(8,128)} %copy-done) | copy-start | bytes 1572868
  253.6 1.0 copy-start.3
  253.6 1.2 copy-start.5
  253.6 1.4 copy-start.6
Sparse Core Ops, SparseCore 0:
  23.9 91.3 reduce-scatter.1
where the time goes:
time: 278 us; the launch traced here: 277 us
  waiting for transfers between devices  159 us (57%)
  other arithmetic  31.6 us (11%)
  starting transfers between devices  28.4 us (10%)
  matrix products  21.8 us (8%)
  between operations  14.9 us (5%)
  local copies, waits for them, and re-layouts  10.7 us (4%)
  blocking collectives  10.3 us (4%)
    reduce_scatter x1, waiting for transfers between devices, per_device(): lax.psum_scatter(partial_value, 'band', scatter_dimension=1, tiled=True)  91.5 us
    all_to_all x2, waiting for transfers between devices, pencil_axes(): lax.all_to_all(second, 'band', split_axis=1, concat_axis=2, tiled=True)  24.2 us
    all_to_all x2, waiting for transfers between devices, pencil_axes(): lax.all_to_all(along_second(lax.all_to_all(second, 'band', split_axis=1,...  22.7 us
    dot_general x2, matrix products, along_third(): return jnp.einsum('fxyl,jl->fxyj', stack, table, precision=EXACT)  16.8 us
    reduce_sum x1, other arithmetic, per_device(): jnp.sum(weights[:, None, None, None] * values * values, axis=0)  14 us
    all_to_all x2, waiting for transfers between devices, pencil_axes(): lax.all_to_all(along_first(lax.all_to_all(first, 'grid', split_axis=2, co...  11.3 us
    all_to_all x1, blocking collectives, pencil_axes(): lax.all_to_all(first, 'grid', split_axis=2, concat_axis=1, tiled=True)  10.3 us
    all_to_all x2, starting transfers between devices, pencil_axes(): lax.all_to_all(along_second(lax.all_to_all(second, 'band', split_axis=1,...  9.29 us
  transfers between devices with their start and end apart: 9, of which 9 were waited for; matrix products, arithmetic and copies ran while one was open for 5% of the time, Pallas kernels for 0%

commit v1 on v0

v1 whole, which is shorter than its diff:
```python
import functools
import math

import jax
import jax.numpy as jnp
import numpy as np
from jax import lax
from jax.experimental import pallas as pl
from jax.experimental.pallas import tpu as pltpu
from jax.sharding import PartitionSpec as P

KAPPA = 0.804
MU_X = 0.2195149727645171
BETA = 0.06672455060314922
GAMMA = (1.0 - math.log(2.0)) / math.pi**2
FZ_NORM = 2.0 ** (4.0 / 3.0) - 2.0
FPP_ZERO = 1.709921
EXACT = lax.Precision.HIGHEST
MESH = pl.DeviceIdType.MESH
CHUNK = 4
FAST = 2


def cube_root(value):
    return jnp.exp(jnp.log(value) * (1.0 / 3.0))


def pw_fit(radius, root, amp, alpha, beta_one, beta_two, beta_three, beta_four):
    denom = (2.0 * amp) * (
        root * (beta_one + root * (beta_two + root * (beta_three + root * beta_four)))
    )
    return -2.0 * amp * (1.0 + alpha * radius) * jnp.log(1.0 + 1.0 / denom)


def exchange_part(double, sigma_four):
    kfermi = (3.0 * math.pi**2) ** (1.0 / 3.0) * cube_root(double)
    product = kfermi * double
    scaled = sigma_four / (4.0 * product * product)
    enhance = 1.0 + KAPPA - KAPPA / (1.0 + MU_X * scaled / KAPPA)
    return -0.75 / math.pi * product * enhance


def xc_energy(n_up, n_down, s_uu, s_ud, s_dd):
    exch = 0.5 * (exchange_part(2.0 * n_up, 4.0 * s_uu) + exchange_part(2.0 * n_down, 4.0 * s_dd))
    total = n_up + n_down
    zeta = (n_up - n_down) / total
    third = cube_root(total)
    radius = (3.0 / (4.0 * math.pi)) ** (1.0 / 3.0) / third
    root = jnp.sqrt(radius)
    ec_para = pw_fit(radius, root, 0.031091, 0.2137, 7.5957, 3.5876, 1.6382, 0.49294)
    ec_ferro = pw_fit(radius, root, 0.015545, 0.20548, 14.1189, 6.1977, 3.3662, 0.62517)
    neg_stiff = pw_fit(radius, root, 0.016887, 0.11125, 10.357, 3.6231, 0.88026, 0.49671)
    plus_z = 1.0 + zeta
    minus_z = 1.0 - zeta
    plus_third = cube_root(plus_z)
    minus_third = cube_root(minus_z)
    fzeta = (plus_z * plus_third + minus_z * minus_third - 2.0) * (1.0 / FZ_NORM)
    zeta_sq = zeta * zeta
    zeta_four = zeta_sq * zeta_sq
    ec_lda = (
        ec_para
        - neg_stiff * fzeta * (1.0 / FPP_ZERO) * (1.0 - zeta_four)
        + (ec_ferro - ec_para) * fzeta * zeta_four
    )
    phi = 0.5 * (plus_third * plus_third + minus_third * minus_third)
    phi_cube = phi * phi * phi
    kfermi = (3.0 * math.pi**2) ** (1.0 / 3.0) * third
    screen_sq = kfermi * (4.0 / math.pi)
    sigma = s_uu + 2.0 * s_ud + s_dd
    tsq = sigma / (4.0 * phi * phi * screen_sq * total * total)
    amp = BETA / GAMMA / (jnp.exp(-ec_lda / (GAMMA * phi_cube)) - 1.0)
    atsq = amp * tsq
    gradient_term = (
        GAMMA
        * phi_cube
        * jnp.log(1.0 + BETA / GAMMA * tsq * (1.0 + atsq) / (1.0 + atsq + atsq * atsq))
    )
    return exch + total * (ec_lda + gradient_term)


def spectral_table(length):
    index = np.arange(length)
    angle = 2.0 * np.pi / length * (index[:, None] * index[None, :] % length)
    mode = np.where(index < length // 2, index, index - length)
    mode = np.where(index == length // 2, 0, mode)
    wave = 2.0 * np.pi / length * mode
    sines, cosines = np.sin(angle), np.cos(angle)
    first_term = (sines * wave[None, :]) @ cosines.T
    second_term = (cosines * wave[None, :]) @ sines.T
    return ((second_term - first_term) / length).astype(np.float32)


def greet(partners):
    barrier = pltpu.get_barrier_semaphore()
    for partner in partners:
        pl.semaphore_signal(barrier, inc=1, device_id=partner, device_id_type=MESH)
    pl.semaphore_wait(barrier, len(partners))


def density_kernel(
    bands,
    pairs_ref,
    orb_hbm,
    core_hbm,
    out_ref,
    orb,
    core,
    part,
    x_in,
    z_out,
    z_in,
    orb_sem,
    core_sem,
    x_send,
    x_recv,
    z_send,
    z_recv,
):
    count, rows, y_cells, z_cells = orb.shape
    block = core.shape[1]
    slow = bands // FAST
    chunks = rows // CHUNK
    me = lax.axis_index("band")
    my_slow, my_fast = lax.div(me, FAST), lax.rem(me, FAST)
    partner = {"band": my_slow * FAST + (1 - my_fast)}
    others = [{"band": lax.rem(my_slow + k, slow) * FAST + my_fast} for k in range(1, slow)]

    def orb_copy(c):
        span = pl.ds(c * CHUNK, CHUNK)
        return pltpu.make_async_copy(orb_hbm.at[0, :, span], orb.at[:, span], orb_sem.at[c])

    def core_copy():
        span = pl.ds(pl.multiple_of(me * block, block), block)
        return pltpu.make_async_copy(core_hbm.at[:, span], core, core_sem)

    def x_copy(c):
        span = pl.ds(c * CHUNK, CHUNK)
        return pltpu.make_async_remote_copy(
            src_ref=part.at[1 - my_fast, span],
            dst_ref=x_in.at[span],
            send_sem=x_send.at[c],
            recv_sem=x_recv.at[c],
            device_id=partner,
            device_id_type=MESH,
        )

    def z_copy(c, k):
        span = pl.ds(c * CHUNK, CHUNK)
        return pltpu.make_async_remote_copy(
            src_ref=z_out.at[lax.rem(my_slow + k, slow), span],
            dst_ref=z_in.at[k - 1, span],
            send_sem=z_send.at[k - 1, c],
            recv_sem=z_recv.at[k - 1, c],
            device_id=others[k - 1],
            device_id_type=MESH,
        )

    def each(body):
        lax.fori_loop(0, chunks, lambda c, carry: (body(c), carry)[1], 0)

    each(lambda c: orb_copy(c).start())
    core_copy().start()
    greet([partner] + others)
    first = pairs_ref[0, 0]
    last = first + pairs_ref[0, 1]
    weights = []
    for n in range(count):
        ident = me * count + n
        weights.append(jnp.where((ident >= first) & (ident < last), 0.5, 1.0).astype(jnp.float32))

    def density(c):
        orb_copy(c).wait()
        for r in range(CHUNK):
            row = c * CHUNK + r
            for piece in range(bands):
                total = jnp.zeros((block, z_cells), jnp.float32)
                for n in range(count):
                    values = orb[n, row, piece * block : (piece + 1) * block].astype(jnp.float32)
                    total += weights[n] * (values * values)
                part[piece % FAST, row, piece // FAST] = total
        x_copy(c).start()

    each(density)

    def forward(c):
        x_copy(c).wait_recv()
        span = pl.ds(c * CHUNK, CHUNK)
        for piece in range(slow):
            z_out[piece, span] = part[my_fast, span, piece] + x_in[span, piece]
        for k in range(1, slow):
            z_copy(c, k).start()

    each(forward)
    core_copy().wait()

    def collect(c):
        span = pl.ds(c * CHUNK, CHUNK)
        total = 0.5 * core[span] + z_out[my_slow, span]
        for k in range(1, slow):
            z_copy(c, k).wait_recv()
            total += z_in[k - 1, span]
        out_ref[span] = total

    each(collect)

    def drain(c):
        x_copy(c).wait_send()
        for k in range(1, slow):
            z_copy(c, k).wait_send()

    each(drain)


def own_density(orbitals, partial_bands, core_density):
    bands = lax.axis_size("band")
    _, count, rows, y_cells, z_cells = orbitals.shape
    block = y_cells // bands
    slow = bands // FAST
    chunks = rows // CHUNK
    return pl.pallas_call(
        functools.partial(density_kernel, bands),
        out_shape=jax.ShapeDtypeStruct((rows, block, z_cells), jnp.float32),
        in_specs=[
            pl.BlockSpec(memory_space=pltpu.SMEM),
            pl.BlockSpec(memory_space=pl.ANY),
            pl.BlockSpec(memory_space=pl.ANY),
        ],
        out_specs=pl.BlockSpec(memory_space=pltpu.VMEM),
        scratch_shapes=[
            pltpu.VMEM((count, rows, y_cells, z_cells), jnp.bfloat16),
            pltpu.VMEM((rows, block, z_cells), jnp.float32),
            pltpu.VMEM((FAST, rows, slow, block, z_cells), jnp.float32),
            pltpu.VMEM((rows, slow, block, z_cells), jnp.float32),
            pltpu.VMEM((slow, rows, block, z_cells), jnp.float32),
            pltpu.VMEM((slow - 1, rows, block, z_cells), jnp.float32),
            pltpu.SemaphoreType.DMA((chunks,)),
            pltpu.SemaphoreType.DMA,
            pltpu.SemaphoreType.DMA((chunks,)),
            pltpu.SemaphoreType.DMA((chunks,)),
            pltpu.SemaphoreType.DMA((slow - 1, chunks)),
            pltpu.SemaphoreType.DMA((slow - 1, chunks)),
        ],
        compiler_params=pltpu.CompilerParams(
            collective_id=0, has_side_effects=True, vmem_limit_bytes=48 * 2**20
        ),
        name="band_density",
    )(partial_bands, orbitals, core_density)


def swapped(block, axis, stride):
    count = lax.axis_size(axis)
    route = []
    for low in range(count):
        high = low | 1 << stride
        if high != low and high < count:
            route += [(low, high), (high, low)]
    return lax.ppermute(block, axis, route)


def along_first(stack, table):
    return jnp.einsum("jl,flyz->fjyz", table, stack, precision=EXACT)


def along_second(stack, table):
    return jnp.einsum("jl,fxlz->fxjz", table, stack, precision=EXACT)


def along_third(stack, table):
    return jnp.einsum("fxyl,jl->fxyj", stack, table, precision=EXACT)


def pencil_axes(first, second, third, tables):
    deriv_x = lax.all_to_all(
        along_first(
            lax.all_to_all(first, "grid", split_axis=2, concat_axis=1, tiled=True), tables[0]
        ),
        "grid",
        split_axis=1,
        concat_axis=2,
        tiled=True,
    )
    deriv_y = lax.all_to_all(
        along_second(
            lax.all_to_all(second, "band", split_axis=1, concat_axis=2, tiled=True), tables[1]
        ),
        "band",
        split_axis=2,
        concat_axis=1,
        tiled=True,
    )
    return (deriv_x, deriv_y, along_third(third, tables[2]))


def per_device(orbitals, partial_bands, core_density):
    x_rows, y_cols, z_cells = core_density.shape
    tables = (
        jnp.asarray(spectral_table(x_rows * lax.axis_size("grid"))),
        jnp.asarray(spectral_table(y_cols)),
        jnp.asarray(spectral_table(z_cells)),
    )
    own = own_density(orbitals, partial_bands, core_density)
    single = own[None]
    steep = jnp.concatenate(pencil_axes(single, single, single, tables), axis=0)
    sent = jnp.concatenate([single, steep], axis=0)
    got = swapped(sent, "spin", 0)
    other = got[0]
    other_steep = got[1:]
    is_up = lax.axis_index("spin") == 0
    dens_up = jnp.where(is_up, own, other)
    dens_down = jnp.where(is_up, other, own)
    grad_up = jnp.where(is_up, steep, other_steep)
    grad_down = jnp.where(is_up, other_steep, steep)
    s_uu = jnp.sum(grad_up * grad_up, axis=0)
    s_ud = jnp.sum(grad_up * grad_down, axis=0)
    s_dd = jnp.sum(grad_down * grad_down, axis=0)
    energy, pull = jax.vjp(xc_energy, dens_up, dens_down, s_uu, s_ud, s_dd)
    derivs = pull(jnp.ones_like(energy))
    dn_own = jnp.where(is_up, derivs[0], derivs[1])
    ds_own = jnp.where(is_up, derivs[2], derivs[4])
    flux = 2.0 * ds_own[None] * steep + derivs[3][None] * other_steep
    div_x, div_y, div_z = pencil_axes(flux[0:1], flux[1:2], flux[2:3], tables)
    potential = dn_own - (div_x[0] + div_y[0] + div_z[0])
    return potential[None]


def solution(mesh):
    in_specs = (P("spin", "band", "grid", None, None), P("spin", None), P("grid", None, None))
    out_specs = P("spin", "grid", "band", None)
    return jax.shard_map(
        per_device, mesh=mesh, in_specs=in_specs, out_specs=out_specs, check_vma=False
    )
```

time: 278 us -> 204 us (0.73)
  waiting for transfers between devices: 159 us -> 66.7 us
  Pallas kernels: 0 us -> 59.5 us
  other arithmetic: 31.6 us -> 11.4 us
  between operations: 14.9 us -> 0.26 us
  matrix products: 21.8 us -> 15.9 us
    reduce_scatter x1 -> x0, waiting for transfers between devices: 91.5 us -> none  [per_device(): lax.psum_scatter(partial_value, 'band', scatter_dimension=1, tiled=True)]
    pallas_call x0 -> x1, Pallas kernels: none -> 59.5 us  [own_density(): pl.pallas_call(functools.partial(density_kernel, bands), out_shape=jax.Sh...]
    reduce_sum x1 -> x0, other arithmetic: 14 us -> none  [per_device(): jnp.sum(weights[:, None, None, None] * values * values, axis=0)]
    dot_general x2, matrix products: 16.8 us -> 11.9 us  [along_third(): return jnp.einsum('fxyl,jl->fxyj', stack, table, precision=EXACT)]
    mul x1, other arithmetic: 8.55 us -> 5.01 us  [per_device(): flux = 2.0 * ds_own[None] * steep + derivs[3][None] * other_steep]
  transfers between devices with their start and end apart: 9 -> 8, of which waited for: 9 -> 8; matrix products, arithmetic and copies ran while one was open for 5% -> 6% of each run, Pallas kernels for 0% -> 0%
where the time goes in v1:
time: 204 us; the launch traced here: 203 us
  waiting for transfers between devices  66.7 us (33%)
  Pallas kernels  59.5 us (29%)
  starting transfers between devices  27.9 us (14%)
  matrix products  15.9 us (8%)
  local copies, waits for them, and re-layouts  12 us (6%)
  other arithmetic  11.4 us (6%)
  blocking collectives  9.3 us (5%)
    pallas_call x1, Pallas kernels, own_density(): pl.pallas_call(functools.partial(density_kernel, bands), out_shape=jax.Sh...  59.5 us
    all_to_all x2, waiting for transfers between devices, pencil_axes(): lax.all_to_all(second, 'band', split_axis=1, concat_axis=2, tiled=True)  23.8 us
    all_to_all x2, waiting for transfers between devices, pencil_axes(): lax.all_to_all(along_second(lax.all_to_all(second, 'band', split_axis=1,...  22.4 us
    dot_general x2, matrix products, along_third(): return jnp.einsum('fxyl,jl->fxyj', stack, table, precision=EXACT)  11.9 us
    all_to_all x2, waiting for transfers between devices, pencil_axes(): lax.all_to_all(along_first(lax.all_to_all(first, 'grid', split_axis=2, co...  10.9 us
    all_to_all x1, blocking collectives, pencil_axes(): lax.all_to_all(first, 'grid', split_axis=2, concat_axis=1, tiled=True)  9.3 us
    all_to_all x2, starting transfers between devices, pencil_axes(): lax.all_to_all(along_second(lax.all_to_all(second, 'band', split_axis=1,...  9.07 us
    all_to_all x2, starting transfers between devices, pencil_axes(): lax.all_to_all(second, 'band', split_axis=1, concat_axis=2, tiled=True)  8.16 us
  transfers between devices with their start and end apart: 8, of which 8 were waited for; matrix products, arithmetic and copies ran while one was open for 6% of the time, Pallas kernels for 0%

profile of v1, /device:TPU:0, one launch (start us, length us, event | category | flops | bytes accessed | tf_op | source)
XLA Modules:
  0.0 202.9 jit_solution(9067580062711523267)
XLA Ops:
  0.0 0.0 copy-start
  0.0 2.2 %copy-done = f32[64,128,128]{2,1,0:T(8,128)S(1)} copy-done((f32[64,128,128]{2,1,0:T(8,128)S(1)}, f32[64,128,128]{2,1,0:T(8,128)}, u32[]{:S(2)}) %copy-start) | copy-done | bytes 4194328
  2.2 0.0 copy-start.1
  2.2 0.7 copy-done.1
  2.8 59.5 %band_density.1 = f32[64,16,128]{2,1,0:T(8,128)} custom-call(s32[1,2]{1,0:T(1,128)S(1)} %copy-done.1, bf16[1,8,64,128,128]{4,3,2,1,0:T(8,128)(2,1)} %orb_hbm.1, f32[64,128,128]{2,1,0:T(8,128)S(1)} %copy-done), custom_call_target="tpu_custom_call" | custom-call | tf_op jit(solution)/shard_map/band_density/pallas_call | solution.py:220
  62.4 1.2 copy.45
  63.6 0.0 copy-start.9
  63.6 9.3 %all_to_all.126 = f32[1,64,16,128]{3,1,0,2:T(8,128)S(1)} all-to-all(f32[1,64,16,128]{3,1,0,2:T(8,128)S(1)} %copy.45), channel_id=1, replica_groups=mesh['spin'=2,'band'=8,'grid'=2] {'grid'}, dimensions={2} | all-to-all | bytes 1048576 | tf_op jit(solution)/shard_map/all_to_all | solution.py:275
  72.9 4.5 %all-to-all-start.2 = ((f32[1,64,16,128]{3,2,0,1:T(8,128)}), f32[1,64,16,128]{3,2,0,1:T(8,128)S(1)}, u32[]{:S(2)}, u32[]{:S(2)}) async-start(f32[1,64,16,128]{3,2,0,1:T(8,128)} %bitcast.8), calls=%async_computation.2 | async-start | bytes 1048576 | tf_op jit(solution)/shard_map/all_to_all | solution.py:284
  77.4 0.3 copy.46
  77.7 0.0 copy-done.9
  77.7 1.0 convolution_bitcast_fusion.4
  78.7 0.0 copy-start.2
  78.7 1.0 copy.48
  79.7 10.0 %all-to-all-done.2 = f32[1,64,16,128]{3,2,0,1:T(8,128)S(1)} async-done(((f32[1,64,16,128]{3,2,0,1:T(8,128)}), f32[1,64,16,128]{3,2,0,1:T(8,128)S(1)}, u32[]{:S(2)}, u32[]{:S(2)}) %all-to-all-start.2) | async-done | bytes 524320 | tf_op jit(solution)/shard_map/all_to_all | solution.py:284
  89.7 3.5 %all-to-all-start.1 = ((f32[1,128,8,128]{3,2,0,1:T(8,128)}), f32[1,128,8,128]{3,2,0,1:T(8,128)S(1)}, u32[]{:S(2)}, u32[]{:S(2)}) async-start(f32[1,128,8,128]{3,2,0,1:T(8,128)} %copy.48), calls=%async_computation.1 | async-start | bytes 1048576 | tf_op jit(solution)/shard_map/all_to_all | solution.py:273
  93.2 0.0 copy-done.2
  93.2 1.0 convolution_bitcast_fusion.3
  94.2 1.0 copy.53
  95.2 4.5 %all-to-all-done.1 = f32[1,128,8,128]{3,2,0,1:T(8,128)S(1)} async-done(((f32[1,128,8,128]{3,2,0,1:T(8,128)}), f32[1,128,8,128]{3,2,0,1:T(8,128)S(1)}, u32[]{:S(2)}, u32[]{:S(2)}) %all-to-all-start.1) | async-done | bytes 524320 | tf_op jit(solution)/shard_map/all_to_all | solution.py:273
  99.7 4.2 %all-to-all-start.3 = ((f32[1,8,128,128]{3,1,0,2:T(8,128)}), f32[1,8,128,128]{3,1,0,2:T(8,128)S(1)}, u32[]{:S(2)}, u32[]{:S(2)}) async-start(f32[1,8,128,128]{3,1,0,2:T(8,128)} %copy.53), calls=%async_computation.3 | async-start | bytes 1048576 | tf_op jit(solution)/shard_map/all_to_all | solution.py:282
  103.9 1.6 convolution_bitcast_fusion.2
  105.6 10.8 %all-to-all-done.3 = f32[1,8,128,128]{3,1,0,2:T(8,128)S(1)} async-done(((f32[1,8,128,128]{3,1,0,2:T(8,128)}), f32[1,8,128,128]{3,1,0,2:T(8,128)S(1)}, u32[]{:S(2)}, u32[]{:S(2)}) %all-to-all-start.3) | async-done | bytes 524320 | tf_op jit(solution)/shard_map/all_to_all | solution.py:282
  116.4 0.1 copy.54
  116.5 2.5 %pad_maximum_fusion = f32[4,64,16,128]{3,2,1,0:T(8,128)} fusion(f32[1,64,16,128]{3,2,1,0:T(8,128)S(1)} %convolution_bitcast_fusion.2, f32[1,64,16,128]{3,2,1,0:T(8,128)S(1)} %bitcast.91, f32[1,64,16,128]{3,2,1,0:T(8,128)S(1)} %bitcast.88, f32[1,64,16,128]{3,2,1,0:T(8,128)} %bitcast), kind=kLoop, calls=%fused_computation | loop fusion | flops 1572864 | bytes 4194304 | tf_op jit(solution)/shard_map/concatenate | solution.py:304
  119.0 0.0 collective-permute-start
  119.0 4.5 %collective-permute-done = f32[4,64,16,128]{3,2,1,0:T(8,128)} collective-permute-done((f32[4,64,16,128]{3,2,1,0:T(8,128)}, f32[4,64,16,128]{3,2,1,0:T(8,128)}, u32[]{:S(2)}, u32[]{:S(2)}) %collective-permute-start) | collective-permute-done | bytes 2097184 | tf_op jit(solution)/shard_map/ppermute | solution.py:257
  123.5 2.1 %multiply_reduce_fusion.1 = (f32[64,16,128]{2,1,0:T(8,128)S(1)}, f32[64,16,128]{2,1,0:T(8,128)S(1)}, f32[64,16,128]{2,1,0:T(8,128)S(1)}) fusion(f32[4,64,16,128]{3,2,1,0:T(8,128)} %collective-permute-done, f32[1,64,16,128]{3,2,1,0:T(8,128)S(1)} %convolution_bitcast_fusion.2, f32[1,64,16,128]{3,2,1,0:T(8,128)S(1)} %bitcast.92, ...), kind=kLoop, calls=%fused_computation.4 | loop fusion | flops 3538944 | bytes 4718593 | tf_op jit(solution)/shard_map/reduce_sum | solution.py:314
  125.6 0.0 copy-start.3
  125.6 0.0 copy-start.5
  125.6 0.0 copy-start.7
  125.7 5.0 %select_multiply_fusion = (f32[64,16,128]{2,1,0:T(8,128)S(1)}, f32[64,16,128]{2,1,0:T(8,128)S(1)}) fusion(f32[64,16,128]{2,1,0:T(8,128)S(1)} %get-tuple-element.7, f32[64,16,128]{2,1,0:T(8,128)S(1)} %get-tuple-element.6, pred[]{:T(512)S(6)} %eq.3, f32[64,16,128]{2,1,0:T(8,128)} %band_density.1, f32[4,64,16,128]{3,2,1,0:T(8,128)} %collective-permute-done, ...), kind=kLoop, calls=%fused_computation.53 | loop fusion | flops 21102592 | bytes 3670017 | tf_op jit(solution)/shard_map/mul | solution.py:320
  130.7 0.0 copy-done.3
  130.7 0.0 copy-done.5
  130.7 0.0 copy-done.7
  130.7 1.7 multiply_add_fusion
  132.4 0.9 fusion.55
  133.3 3.7 %all-to-all-start.6 = ((f32[1,64,16,128]{3,2,0,1:T(8,128)}), f32[1,64,16,128]{3,2,0,1:T(8,128)S(1)}, u32[]{:S(2)}, u32[]{:S(2)}) async-start(f32[1,64,16,128]{3,2,0,1:T(8,128)} %get-tuple-element.11), calls=%async_computation.6 | async-start | bytes 1048576 | tf_op jit(solution)/shard_map/all_to_all | solution.py:284
  137.0 1.0 copy.56
  137.9 13.9 %all-to-all-done.6 = f32[1,64,16,128]{3,2,0,1:T(8,128)S(1)} async-done(((f32[1,64,16,128]{3,2,0,1:T(8,128)}), f32[1,64,16,128]{3,2,0,1:T(8,128)S(1)}, u32[]{:S(2)}, u32[]{:S(2)}) %all-to-all-start.6) | async-done | bytes 524320 | tf_op jit(solution)/shard_map/all_to_all | solution.py:284
  151.8 3.5 %all-to-all-start.4 = ((f32[1,64,16,128]{3,1,0,2:T(8,128)}), f32[1,64,16,128]{3,1,0,2:T(8,128)S(1)}, u32[]{:S(2)}, u32[]{:S(2)}) async-start(f32[1,64,16,128]{3,1,0,2:T(8,128)} %copy.56), calls=%async_computation.4 | async-start | bytes 1048576 | tf_op jit(solution)/shard_map/all_to_all | solution.py:275
  155.3 1.0 convolution_bitcast_fusion
  156.3 1.0 copy.64
  157.3 5.1 %all-to-all-done.4 = f32[1,64,16,128]{3,1,0,2:T(8,128)S(1)} async-done(((f32[1,64,16,128]{3,1,0,2:T(8,128)}), f32[1,64,16,128]{3,1,0,2:T(8,128)S(1)}, u32[]{:S(2)}, u32[]{:S(2)}) %all-to-all-start.4) | async-done | bytes 524320 | tf_op jit(solution)/shard_map/all_to_all | solution.py:275
  162.4 4.9 %all-to-all-start.7 = ((f32[1,8,128,128]{3,1,0,2:T(8,128)}), f32[1,8,128,128]{3,1,0,2:T(8,128)S(1)}, u32[]{:S(2)}, u32[]{:S(2)}) async-start(f32[1,8,128,128]{3,1,0,2:T(8,128)} %copy.64), calls=%async_computation.7 | async-start | bytes 1048576 | tf_op jit(solution)/shard_map/all_to_all | solution.py:282
  167.3 0.3 copy.57
  167.6 1.0 convolution_bitcast_fusion.1
  168.6 1.0 copy.59
  169.6 11.5 %all-to-all-done.7 = f32[1,8,128,128]{3,1,0,2:T(8,128)S(1)} async-done(((f32[1,8,128,128]{3,1,0,2:T(8,128)}), f32[1,8,128,128]{3,1,0,2:T(8,128)S(1)}, u32[]{:S(2)}, u32[]{:S(2)}) %all-to-all-start.7) | async-done | bytes 524320 | tf_op jit(solution)/shard_map/all_to_all | solution.py:282
  181.2 3.7 %all-to-all-start.5 = ((f32[1,128,8,128]{3,2,0,1:T(8,128)}), f32[1,128,8,128]{3,2,0,1:T(8,128)S(1)}, u32[]{:S(2)}, u32[]{:S(2)}) async-start(f32[1,128,8,128]{3,2,0,1:T(8,128)} %copy.59), calls=%async_computation.5 | async-start | bytes 1048576 | tf_op jit(solution)/shard_map/all_to_all | solution.py:273
  184.8 0.1 copy.65
  185.0 0.0 copy-start.4
  185.0 6.4 %all-to-all-done.5 = f32[1,128,8,128]{3,2,0,1:T(8,128)S(1)} async-done(((f32[1,128,8,128]{3,2,0,1:T(8,128)}), f32[1,128,8,128]{3,2,0,1:T(8,128)S(1)}, u32[]{:S(2)}, u32[]{:S(2)}) %all-to-all-start.5) | async-done | bytes 524320 | tf_op jit(solution)/shard_map/all_to_all | solution.py:273
  191.4 0.0 copy-start.6
  191.4 0.0 copy-start.8
  191.4 0.1 bitcast_add_fusion
  191.5 0.0 copy-done.4
  191.5 1.0 copy-done.6
  192.5 0.2 copy-done.8
  192.6 10.3 %fusion.1 = f32[1,64,16,128]{3,2,1,0:T(8,128)} fusion(f32[64,16,128]{2,1,0:T(8,128)S(1)} %bitcast_add_fusion, f32[128,128,1]{1,0,2:T(8,128)S(1)} %copy-done.2, f32[3,64,16,128]{3,2,1,0:T(8,128)S(1)} %multiply_add_fusion, f32[64,16,128]{2,1,0:T(8,128)S(1)} %copy-done.6, f32[64,16,128]{2,1,0:T(8,128)S(1)} %copy-done.8, f32[64,16,128]{2,1,0:T(8,128)S(1)} %copy-done.4, ...), kind=kOutput, calls=%fused_computation.15 | convolution fusion | flops 249692160 | bytes 4259841 | tf_op jit(solution)/shard_map/fxyl,jl->fxyj/dot_general | solution.py:269
  (6 shorter events, 0.2 us)
Async XLA Ops:
  0.0 2.2 %copy-start = (f32[64,128,128]{2,1,0:T(8,128)S(1)}, f32[64,128,128]{2,1,0:T(8,128)}, u32[]{:S(2)}) copy-start(f32[64,128,128]{2,1,0:T(8,128)} %core_hbm.1) | copy-start | bytes 12582916
  2.2 0.7 copy-start.1
  63.6 14.1 %copy-start.9 = (f32[128,128,1]{1,0,2:T(8,128)S(1)}, f32[128,128,1]{1,0,2:T(8,128)}, u32[]{:S(2)}) copy-start(f32[128,128,1]{1,0,2:T(8,128)} %constant.118) | copy-start | bytes 196612
  72.9 16.8 %all-to-all-start.2 = ((f32[1,64,16,128]{3,2,0,1:T(8,128)}), f32[1,64,16,128]{3,2,0,1:T(8,128)S(1)}, u32[]{:S(2)}, u32[]{:S(2)}) async-start(f32[1,64,16,128]{3,2,0,1:T(8,128)} %bitcast.8), calls=%async_computation.2 | async-start | bytes 1048576 | tf_op jit(solution)/shard_map/all_to_all | solution.py:284
  78.7 14.5 %copy-start.2 = (f32[128,128,1]{1,0,2:T(8,128)S(1)}, f32[128,128,1]{1,0,2:T(8,128)}, u32[]{:S(2)}) copy-start(f32[128,128,1]{1,0,2:T(8,128)} %constant.119) | copy-start | bytes 196612
  89.7 10.1 %all-to-all-start.1 = ((f32[1,128,8,128]{3,2,0,1:T(8,128)}), f32[1,128,8,128]{3,2,0,1:T(8,128)S(1)}, u32[]{:S(2)}, u32[]{:S(2)}) async-start(f32[1,128,8,128]{3,2,0,1:T(8,128)} %copy.48), calls=%async_computation.1 | async-start | bytes 1048576 | tf_op jit(solution)/shard_map/all_to_all | solution.py:273
  99.7 16.7 %all-to-all-start.3 = ((f32[1,8,128,128]{3,1,0,2:T(8,128)}), f32[1,8,128,128]{3,1,0,2:T(8,128)S(1)}, u32[]{:S(2)}, u32[]{:S(2)}) async-start(f32[1,8,128,128]{3,1,0,2:T(8,128)} %copy.53), calls=%async_computation.3 | async-start | bytes 1048576 | tf_op jit(solution)/shard_map/all_to_all | solution.py:282
  119.0 4.5 %collective-permute-start = (f32[4,64,16,128]{3,2,1,0:T(8,128)}, f32[4,64,16,128]{3,2,1,0:T(8,128)}, u32[]{:S(2)}, u32[]{:S(2)}) collective-permute-start(f32[4,64,16,128]{3,2,1,0:T(8,128)} %pad_maximum_fusion), channel_id=1, source_target_pairs={{0,16},{16,0},{1,17},{17,1},{2,18},{18,2},{3,19},{19,3},{4,20},{20... | collective-permute-start | bytes 6291464 | tf_op jit(solution)/shard_map/ppermute | solution.py:257
  125.6 5.0 %copy-start.3 = (f32[64,16,128]{2,1,0:T(8,128)}, f32[64,16,128]{2,1,0:T(8,128)S(1)}, u32[]{:S(2)}) copy-start(f32[64,16,128]{2,1,0:T(8,128)S(1)} %get-tuple-element.5) | copy-start | bytes 1572868
  125.6 5.0 %copy-start.5 = (f32[64,16,128]{2,1,0:T(8,128)}, f32[64,16,128]{2,1,0:T(8,128)S(1)}, u32[]{:S(2)}) copy-start(f32[64,16,128]{2,1,0:T(8,128)S(1)} %get-tuple-element.6) | copy-start | bytes 1572868
  125.6 5.0 %copy-start.7 = (f32[64,16,128]{2,1,0:T(8,128)}, f32[64,16,128]{2,1,0:T(8,128)S(1)}, u32[]{:S(2)}) copy-start(f32[64,16,128]{2,1,0:T(8,128)S(1)} %get-tuple-element.7) | copy-start | bytes 1572868
  133.3 18.5 %all-to-all-start.6 = ((f32[1,64,16,128]{3,2,0,1:T(8,128)}), f32[1,64,16,128]{3,2,0,1:T(8,128)S(1)}, u32[]{:S(2)}, u32[]{:S(2)}) async-start(f32[1,64,16,128]{3,2,0,1:T(8,128)} %get-tuple-element.11), calls=%async_computation.6 | async-start | bytes 1048576 | tf_op jit(solution)/shard_map/all_to_all | solution.py:284
  151.8 10.6 %all-to-all-start.4 = ((f32[1,64,16,128]{3,1,0,2:T(8,128)}), f32[1,64,16,128]{3,1,0,2:T(8,128)S(1)}, u32[]{:S(2)}, u32[]{:S(2)}) async-start(f32[1,64,16,128]{3,1,0,2:T(8,128)} %copy.56), calls=%async_computation.4 | async-start | bytes 1048576 | tf_op jit(solution)/shard_map/all_to_all | solution.py:275
  162.4 18.7 %all-to-all-start.7 = ((f32[1,8,128,128]{3,1,0,2:T(8,128)}), f32[1,8,128,128]{3,1,0,2:T(8,128)S(1)}, u32[]{:S(2)}, u32[]{:S(2)}) async-start(f32[1,8,128,128]{3,1,0,2:T(8,128)} %copy.64), calls=%async_computation.7 | async-start | bytes 1048576 | tf_op jit(solution)/shard_map/all_to_all | solution.py:282
  181.2 10.3 %all-to-all-start.5 = ((f32[1,128,8,128]{3,2,0,1:T(8,128)}), f32[1,128,8,128]{3,2,0,1:T(8,128)S(1)}, u32[]{:S(2)}, u32[]{:S(2)}) async-start(f32[1,128,8,128]{3,2,0,1:T(8,128)} %copy.59), calls=%async_computation.5 | async-start | bytes 1048576 | tf_op jit(solution)/shard_map/all_to_all | solution.py:273
  185.0 6.5 %copy-start.4 = (f32[64,16,128]{2,1,0:T(8,128)S(1)}, f32[64,16,128]{2,1,0:T(8,128)}, u32[]{:S(2)}) copy-start(f32[64,16,128]{2,1,0:T(8,128)} %copy-done.3) | copy-start | bytes 1572868
  191.4 1.0 copy-start.6
  191.4 1.2 copy-start.8

commit v2 on v1

--- a/solution.py
+++ b/solution.py
@@ -19,6 +19,9 @@
 MESH = pl.DeviceIdType.MESH
 CHUNK = 4
 FAST = 2
+STEPS = 2
+PARTS = 4
+XC_ROWS = 2
 
 
 def cube_root(value):
@@ -247,48 +250,279 @@
     )(partial_bands, orbitals, core_density)
 
 
-def swapped(block, axis, stride):
-    count = lax.axis_size(axis)
-    route = []
-    for low in range(count):
-        high = low | 1 << stride
-        if high != low and high < count:
-            route += [(low, high), (high, low)]
-    return lax.ppermute(block, axis, route)
-
-
-def along_first(stack, table):
-    return jnp.einsum("jl,flyz->fjyz", table, stack, precision=EXACT)
-
-
-def along_second(stack, table):
-    return jnp.einsum("jl,fxlz->fxjz", table, stack, precision=EXACT)
-
-
-def along_third(stack, table):
-    return jnp.einsum("fxyl,jl->fxyj", stack, table, precision=EXACT)
-
-
-def pencil_axes(first, second, third, tables):
-    deriv_x = lax.all_to_all(
-        along_first(
-            lax.all_to_all(first, "grid", split_axis=2, concat_axis=1, tiled=True), tables[0]
+def field_kernel(
+    bands,
+    grids,
+    own_ref,
+    tx_ref,
+    ty_ref,
+    tz_ref,
+    out_ref,
+    line,
+    gx,
+    hx,
+    sx,
+    gy,
+    hy,
+    sy,
+    dx,
+    dz,
+    other,
+    fields,
+    outgoing,
+    xf_send,
+    xf_recv,
+    xb_send,
+    xb_recv,
+    yf_send,
+    yf_recv,
+    yb_send,
+    yb_recv,
+    in_send,
+    in_recv,
+    out_send,
+    out_recv,
+):
+    rows, block, z_cells = own_ref.shape
+    y_part = block // grids
+    r_part = rows // bands
+    steps = yf_send.shape[1]
+    r_step = r_part // steps
+    half = rows // 2
+    parts = out_send.shape[0]
+    p_rows = half // parts
+    me = lax.axis_index("band")
+    slab = lax.axis_index("grid")
+    spin = lax.axis_index("spin")
+    twin = {"spin": 1 - spin}
+    my_block = pl.ds(pl.multiple_of(me * block, 8), block)
+    my_slab = pl.ds(pl.multiple_of(slab * rows, 8), rows)
+    mine = pl.ds(spin * half, half)
+    theirs = pl.ds((1 - spin) * half, half)
+
+    def remote(src, dst, send, recv, device):
+        return pltpu.make_async_remote_copy(
+            src_ref=src,
+            dst_ref=dst,
+            send_sem=send,
+            recv_sem=recv,
+            device_id=device,
+            device_id_type=MESH,
+        )
+
+    def x_forward(t, k):
+        q = lax.rem(slab + k, grids)
+        return remote(
+            line.at[t, pl.ds(q * y_part, y_part)],
+            gx.at[t, :, my_slab],
+            xf_send.at[t, k - 1],
+            xf_recv.at[t, k - 1],
+            {"grid": q},
+        )
+
+    def x_back(t, k):
+        q = lax.rem(slab + k, grids)
+        return remote(
+            hx.at[t, :, pl.ds(pl.multiple_of(q * rows, 8), rows)],
+            sx.at[t, pl.ds(slab * y_part, y_part)],
+            xb_send.at[t, k - 1],
+            xb_recv.at[t, k - 1],
+            {"grid": q},
+        )
+
+    def y_forward(t, s, k):
+        q = lax.rem(me + k, bands)
+        source = own_ref if t == 0 else fields.at[2]
+        return remote(
+            source.at[pl.ds(q * r_part + s * r_step, r_step)],
+            gy.at[t, pl.ds(s * r_step, r_step), my_block],
+            yf_send.at[t, s, k - 1],
+            yf_recv.at[t, s, k - 1],
+            {"band": q},
+        )
+
+    def y_back(t, s, k):
+        q = lax.rem(me + k, bands)
+        return remote(
+            hy.at[t, pl.ds(s * r_step, r_step), pl.ds(pl.multiple_of(q * block, 8), block)],
+            sy.at[t, pl.ds(me * r_part + s * r_step, r_step)],
+            yb_send.at[t, s, k - 1],
+            yb_recv.at[t, s, k - 1],
+            {"band": q},
+        )
+
+    incoming = [own_ref, dz, dx, sy.at[0]]
+
+    def swap_in(f):
+        return remote(
+            incoming[f].at[theirs], other.at[f], in_send.at[f], in_recv.at[f], twin
+        )
+
+    def swap_out(p):
+        return remote(
+            outgoing.at[:, pl.ds(p * p_rows, p_rows)],
+            fields.at[:, pl.ds(spin * half + p * p_rows, p_rows)],
+            out_send.at[p],
+            out_recv.at[p],
+            twin,
+        )
+
+    def times(table, field):
+        return jnp.dot(table, field, precision=EXACT, preferred_element_type=jnp.float32)
+
+    def turned(value):
+        return jnp.transpose(value, (1, 0, 2))
+
+    def along_third(field):
+        flat = field.reshape(rows * block, z_cells)
+        return times(flat, tz_ref[...]).reshape(rows, block, z_cells)
+
+    def start(t):
+        for s in range(steps):
+            for k in range(1, bands):
+                y_forward(t, s, k).start()
+        source = own_ref if t == 0 else fields.at[1]
+        line[t] = turned(source[...])
+        for k in range(1, grids):
+            x_forward(t, k).start()
+        gx[t, :, my_slab] = line[t, pl.ds(slab * y_part, y_part)]
+        y_source = own_ref if t == 0 else fields.at[2]
+        gy[t, :, my_block] = y_source[pl.ds(me * r_part, r_part)]
+
+    def along_first(t):
+        for k in range(1, grids):
+            x_forward(t, k).wait_recv()
+        for y in range(y_part):
+            hx[t, y] = times(tx_ref[...], gx[t, y])
+        for k in range(1, grids):
+            x_back(t, k).start()
+        sx[t, pl.ds(slab * y_part, y_part)] = hx[t, :, my_slab]
+
+    def along_second(t):
+        for s in range(steps):
+            for k in range(1, bands):
+                y_forward(t, s, k).wait_recv()
+            for r in range(s * r_step, (s + 1) * r_step):
+                hy[t, r] = times(ty_ref[...], gy[t, r])
+            for k in range(1, bands):
+                y_back(t, s, k).start()
+        sy[t, pl.ds(me * r_part, r_part)] = hy[t, :, my_block]
+
+    def end_first(t):
+        for k in range(1, grids):
+            x_back(t, k).wait_recv()
+        return turned(sx[t])
+
+    def end_second(t):
+        for s in range(steps):
+            for k in range(1, bands):
+                y_back(t, s, k).wait_recv()
+
+    greet(
+        [twin]
+        + [{"grid": lax.rem(slab + k, grids)} for k in range(1, grids)]
+        + [{"band": lax.rem(me + k, bands)} for k in range(1, bands)]
+    )
+    start(0)
+    swap_in(0).start()
+    dz[...] = along_third(own_ref[...])
+    swap_in(1).start()
+    along_first(0)
+    along_second(0)
+    dx[...] = end_first(0)
+    swap_in(2).start()
+    end_second(0)
+    swap_in(3).start()
+    for f in range(4):
+        swap_in(f).wait_recv()
+
+    def potential_rows(row):
+        here = pl.ds(spin * half + row, XC_ROWS)
+        there = pl.ds(row, XC_ROWS)
+        n_own, n_other = own_ref[here], other[0, there]
+        g_own = [dx[here], sy[0, here], dz[here]]
+        g_other = [other[2, there], other[3, there], other[1, there]]
+        s_own = g_own[0] * g_own[0] + g_own[1] * g_own[1] + g_own[2] * g_own[2]
+        s_mix = g_own[0] * g_other[0] + g_own[1] * g_other[1] + g_own[2] * g_other[2]
+        s_other = g_other[0] * g_other[0] + g_other[1] * g_other[1] + g_other[2] * g_other[2]
+        energy, pull = jax.vjp(xc_energy, n_own, n_other, s_own, s_mix, s_other)
+        derivs = pull(jnp.ones_like(energy))
+        fields[0, here] = derivs[0]
+        outgoing[0, there] = derivs[1]
+        for a in range(3):
+            fields[1 + a, here] = 2.0 * derivs[2] * g_own[a] + derivs[3] * g_other[a]
+            outgoing[1 + a, there] = 2.0 * derivs[4] * g_other[a] + derivs[3] * g_own[a]
+
+    for p in range(parts):
+        lax.fori_loop(
+            0,
+            p_rows // XC_ROWS,
+            lambda i, carry: (potential_rows(p * p_rows + i * XC_ROWS), carry)[1],
+            0,
+        )
+        swap_out(p).start()
+    for p in range(parts):
+        swap_out(p).wait_recv()
+    start(1)
+    along_first(1)
+    out_ref[...] = fields[0] - along_third(fields[3])
+    along_second(1)
+    first = end_first(1)
+    end_second(1)
+    out_ref[...] = out_ref[...] - (first + sy[1])
+
+    for t in range(2):
+        for k in range(1, grids):
+            x_forward(t, k).wait_send()
+            x_back(t, k).wait_send()
+        for s in range(steps):
+            for k in range(1, bands):
+                y_forward(t, s, k).wait_send()
+                y_back(t, s, k).wait_send()
+    for f in range(4):
+        swap_in(f).wait_send()
+    for p in range(parts):
+        swap_out(p).wait_send()
+
+
+def field_potential(own, tables):
+    bands, grids = lax.axis_size("band"), lax.axis_size("grid")
+    rows, block, z_cells = own.shape
+    y_part, r_part = block // grids, rows // bands
+    y_cells, x_cells = block * bands, rows * grids
+    steps = math.gcd(STEPS, r_part)
+    parts = math.gcd(PARTS, rows // 2 // XC_ROWS)
+    vmem = pl.BlockSpec(memory_space=pltpu.VMEM)
+    dma = pltpu.SemaphoreType.DMA
+    real = jnp.float32
+    return pl.pallas_call(
+        functools.partial(field_kernel, bands, grids),
+        out_shape=jax.ShapeDtypeStruct((rows, block, z_cells), real),
+        in_specs=[vmem] * 4,
+        out_specs=vmem,
+        scratch_shapes=[
+            pltpu.VMEM((2, block, rows, z_cells), real),
+            pltpu.VMEM((2, y_part, x_cells, z_cells), real),
+            pltpu.VMEM((2, y_part, x_cells, z_cells), real),
+            pltpu.VMEM((2, block, rows, z_cells), real),
+            pltpu.VMEM((2, r_part, y_cells, z_cells), real),
+            pltpu.VMEM((2, r_part, y_cells, z_cells), real),
+            pltpu.VMEM((2, rows, block, z_cells), real),
+            pltpu.VMEM((rows, block, z_cells), real),
+            pltpu.VMEM((rows, block, z_cells), real),
+            pltpu.VMEM((4, rows // 2, block, z_cells), real),
+            pltpu.VMEM((4, rows, block, z_cells), real),
+            pltpu.VMEM((4, rows // 2, block, z_cells), real),
+        ]
+        + [dma((2, grids - 1))] * 4
+        + [dma((2, steps, bands - 1))] * 4
+        + [dma((4,))] * 2
+        + [dma((parts,))] * 2,
+        compiler_params=pltpu.CompilerParams(
+            collective_id=1, has_side_effects=True, vmem_limit_bytes=32 * 2**20
         ),
-        "grid",
-        split_axis=1,
-        concat_axis=2,
-        tiled=True,
-    )
-    deriv_y = lax.all_to_all(
-        along_second(
-            lax.all_to_all(second, "band", split_axis=1, concat_axis=2, tiled=True), tables[1]
-        ),
-        "band",
-        split_axis=2,
-        concat_axis=1,
-        tiled=True,
-    )
-    return (deriv_x, deriv_y, along_third(third, tables[2]))
+        name="field_potential",
+    )(own, *tables)
 
 
 def per_device(orbitals, partial_bands, core_density):
@@ -296,31 +530,10 @@
     tables = (
         jnp.asarray(spectral_table(x_rows * lax.axis_size("grid"))),
         jnp.asarray(spectral_table(y_cols)),
-        jnp.asarray(spectral_table(z_cells)),
+        jnp.asarray(spectral_table(z_cells).T),
     )
     own = own_density(orbitals, partial_bands, core_density)
-    single = own[None]
-    steep = jnp.concatenate(pencil_axes(single, single, single, tables), axis=0)
-    sent = jnp.concatenate([single, steep], axis=0)
-    got = swapped(sent, "spin", 0)
-    other = got[0]
-    other_steep = got[1:]
-    is_up = lax.axis_index("spin") == 0
-    dens_up = jnp.where(is_up, own, other)
-    dens_down = jnp.where(is_up, other, own)
-    grad_up = jnp.where(is_up, steep, other_steep)
-    grad_down = jnp.where(is_up, other_steep, steep)
-    s_uu = jnp.sum(grad_up * grad_up, axis=0)
-    s_ud = jnp.sum(grad_up * grad_down, axis=0)
-    s_dd = jnp.sum(grad_down * grad_down, axis=0)
-    energy, pull = jax.vjp(xc_energy, dens_up, dens_down, s_uu, s_ud, s_dd)
-    derivs = pull(jnp.ones_like(energy))
-    dn_own = jnp.where(is_up, derivs[0], derivs[1])
-    ds_own = jnp.where(is_up, derivs[2], derivs[4])
-    flux = 2.0 * ds_own[None] * steep + derivs[3][None] * other_steep
-    div_x, div_y, div_z = pencil_axes(flux[0:1], flux[1:2], flux[2:3], tables)
-    potential = dn_own - (div_x[0] + div_y[0] + div_z[0])
-    return potential[None]
+    return field_potential(own, tables)[None]
 
 
 def solution(mesh):

time: 204 us -> 123 us (0.60)
  waiting for transfers between devices: 66.7 us -> 0 us
  Pallas kernels: 59.5 us -> 119 us
  starting transfers between devices: 27.9 us -> 0 us
  matrix products: 15.9 us -> 0 us
  other arithmetic: 11.4 us -> 0 us
  blocking collectives: 9.3 us -> 0 us
  local copies, waits for them, and re-layouts: 12 us -> 3.65 us
    all_to_all x7 -> x0, waiting for transfers between devices: 62.2 us -> none  [the longest x2 23.8 us: pencil_axes(): lax.all_to_all(second, 'band', split_axis=1, concat_axis=2, tiled=True)]
    pallas_call x0 -> x1, Pallas kernels: none -> 60.3 us  [field_potential(): pl.pallas_call(functools.partial(field_kernel, bands, grids), out_shape=j...]
    all_to_all x7 -> x0, starting transfers between devices: 27.9 us -> none  [the longest x2 9.07 us: pencil_axes(): lax.all_to_all(along_second(lax.all_to_all(second, 'band', split_axis=1,...]
    dot_general x6 -> x0, matrix products: 15.9 us -> none  [the longest x2 11.9 us: along_third(): return jnp.einsum('fxyl,jl->fxyj', stack, table, precision=EXACT)]
    all_to_all x1 -> x0, blocking collectives: 9.3 us -> none  [pencil_axes(): lax.all_to_all(first, 'grid', split_axis=2, concat_axis=1, tiled=True)]
    mul x2 -> x0, other arithmetic: 5.04 us -> none  [the longest x1 5.01 us: per_device(): flux = 2.0 * ds_own[None] * steep + derivs[3][None] * other_steep]
    ppermute x1 -> x0, waiting for transfers between devices: 4.5 us -> none  [swapped(): return lax.ppermute(block, axis, route)]
    transpose x4 -> x0, local copies, waits for them, and re-layouts: 3.99 us -> none  [the longest x2 2 us: along_first(): return jnp.einsum('jl,flyz->fjyz', table, stack, precision=EXACT)]
  transfers between devices with their start and end apart: 8 -> 0, of which waited for: 8 -> 0; matrix products, arithmetic and copies ran while one was open for 6% -> 0% of each run, Pallas kernels for 0% -> 0%
where the time goes in v2:
time: 123 us
  Pallas kernels  119 us (97%)
  local copies, waits for them, and re-layouts  3.65 us (3%)
    pallas_call x1, Pallas kernels, field_potential(): pl.pallas_call(functools.partial(field_kernel, bands, grids), out_shape=j...  60.3 us
    pallas_call x1, Pallas kernels, own_density(): pl.pallas_call(functools.partial(density_kernel, bands), out_shape=jax.Sh...  58.7 us
    unnamed x9, local copies, waits for them, and re-layouts  3.65 us

profile of v2, /device:TPU:0, one launch (start us, length us, event | category | flops | bytes accessed | tf_op | source)
XLA Modules:
  0.0 122.7 jit_solution(11605078675237146360)
XLA Ops:
  0.0 0.0 copy-start
  0.0 2.2 %copy-done = f32[64,128,128]{2,1,0:T(8,128)S(1)} copy-done((f32[64,128,128]{2,1,0:T(8,128)S(1)}, f32[64,128,128]{2,1,0:T(8,128)}, u32[]{:S(2)}) %copy-start) | copy-done | bytes 4194328
  2.2 0.0 copy-start.3
  2.2 0.7 copy-done.3
  2.8 0.0 copy-start.1
  2.8 0.0 copy-start.2
  2.8 58.7 %band_density.1.own_ref = f32[64,16,128]{2,1,0:T(8,128)S(1)} custom-call(s32[1,2]{1,0:T(1,128)S(1)} %copy-done.3, bf16[1,8,64,128,128]{4,3,2,1,0:T(8,128)(2,1)} %orb_hbm.1, f32[64,128,128]{2,1,0:T(8,128)S(1)} %copy-done), custom_call_target="tpu_custom_call" | custom-call | tf_op jit(solution)/shard_map/band_density/pallas_call | solution.py:223
  61.6 0.0 copy-done.1
  61.6 0.0 copy-done.2
  61.6 60.3 %field_potential.1 = f32[64,16,128]{2,1,0:T(8,128)S(1)} custom-call(f32[64,16,128]{2,1,0:T(8,128)S(1)} %band_density.1.own_ref, f32[128,128]{1,0:T(8,128)S(1)} %copy-done.1, f32[128,128]{1,0:T(8,128)S(1)} %copy-done.1, f32[128,128]{1,0:T(8,128)S(1)} %copy-done.2), custom_call_target="tpu_custom_call" | custom-call | tf_op jit(solution)/shard_map/field_potential/pallas_call | solution.py:498
  121.9 0.8 copy.8
Async XLA Ops:
  0.0 2.2 %copy-start = (f32[64,128,128]{2,1,0:T(8,128)S(1)}, f32[64,128,128]{2,1,0:T(8,128)}, u32[]{:S(2)}) copy-start(f32[64,128,128]{2,1,0:T(8,128)} %core_hbm.1) | copy-start | bytes 12582916
  2.2 0.7 copy-start.3
  2.8 58.7 %copy-start.1 = (f32[128,128]{1,0:T(8,128)S(1)}, f32[128,128]{1,0:T(8,128)}, u32[]{:S(2)}) copy-start(f32[128,128]{1,0:T(8,128)} %constant.4.clone.tx_ref.ty_ref) | copy-start | bytes 196612
  2.8 58.7 %copy-start.2 = (f32[128,128]{1,0:T(8,128)S(1)}, f32[128,128]{1,0:T(8,128)}, u32[]{:S(2)}) copy-start(f32[128,128]{1,0:T(8,128)} %constant.5.clone.tz_ref) | copy-start | bytes 196612

commit v3 on v1

v3 whole, which is shorter than its diff:
```python
import functools
import math

import jax
import jax.numpy as jnp
import numpy as np
from jax import lax
from jax.experimental import pallas as pl
from jax.experimental.pallas import tpu as pltpu
from jax.sharding import PartitionSpec as P

KAPPA = 0.804
MU_X = 0.2195149727645171
BETA = 0.06672455060314922
GAMMA = (1.0 - math.log(2.0)) / math.pi**2
FZ_NORM = 2.0 ** (4.0 / 3.0) - 2.0
FPP_ZERO = 1.709921
EXACT = lax.Precision.HIGHEST
MESH = pl.DeviceIdType.MESH
CHUNK = 4
FAST = 2
XC_ROWS = 2
TILE = 8


def cube_root(value):
    return jnp.exp(jnp.log(value) * (1.0 / 3.0))


def pw_fit(radius, root, amp, alpha, beta_one, beta_two, beta_three, beta_four):
    denom = (2.0 * amp) * (
        root * (beta_one + root * (beta_two + root * (beta_three + root * beta_four)))
    )
    return -2.0 * amp * (1.0 + alpha * radius) * jnp.log(1.0 + 1.0 / denom)


def exchange_part(double, sigma_four):
    kfermi = (3.0 * math.pi**2) ** (1.0 / 3.0) * cube_root(double)
    product = kfermi * double
    scaled = sigma_four / (4.0 * product * product)
    enhance = 1.0 + KAPPA - KAPPA / (1.0 + MU_X * scaled / KAPPA)
    return -0.75 / math.pi * product * enhance


def xc_energy(n_up, n_down, s_uu, s_ud, s_dd):
    exch = 0.5 * (exchange_part(2.0 * n_up, 4.0 * s_uu) + exchange_part(2.0 * n_down, 4.0 * s_dd))
    total = n_up + n_down
    zeta = (n_up - n_down) / total
    third = cube_root(total)
    radius = (3.0 / (4.0 * math.pi)) ** (1.0 / 3.0) / third
    root = jnp.sqrt(radius)
    ec_para = pw_fit(radius, root, 0.031091, 0.2137, 7.5957, 3.5876, 1.6382, 0.49294)
    ec_ferro = pw_fit(radius, root, 0.015545, 0.20548, 14.1189, 6.1977, 3.3662, 0.62517)
    neg_stiff = pw_fit(radius, root, 0.016887, 0.11125, 10.357, 3.6231, 0.88026, 0.49671)
    plus_z = 1.0 + zeta
    minus_z = 1.0 - zeta
    plus_third = cube_root(plus_z)
    minus_third = cube_root(minus_z)
    fzeta = (plus_z * plus_third + minus_z * minus_third - 2.0) * (1.0 / FZ_NORM)
    zeta_sq = zeta * zeta
    zeta_four = zeta_sq * zeta_sq
    ec_lda = (
        ec_para
        - neg_stiff * fzeta * (1.0 / FPP_ZERO) * (1.0 - zeta_four)
        + (ec_ferro - ec_para) * fzeta * zeta_four
    )
    phi = 0.5 * (plus_third * plus_third + minus_third * minus_third)
    phi_cube = phi * phi * phi
    kfermi = (3.0 * math.pi**2) ** (1.0 / 3.0) * third
    screen_sq = kfermi * (4.0 / math.pi)
    sigma = s_uu + 2.0 * s_ud + s_dd
    tsq = sigma / (4.0 * phi * phi * screen_sq * total * total)
    amp = BETA / GAMMA / (jnp.exp(-ec_lda / (GAMMA * phi_cube)) - 1.0)
    atsq = amp * tsq
    gradient_term = (
        GAMMA
        * phi_cube
        * jnp.log(1.0 + BETA / GAMMA * tsq * (1.0 + atsq) / (1.0 + atsq + atsq * atsq))
    )
    return exch + total * (ec_lda + gradient_term)


def spectral_table(length):
    index = np.arange(length)
    angle = 2.0 * np.pi / length * (index[:, None] * index[None, :] % length)
    mode = np.where(index < length // 2, index, index - length)
    mode = np.where(index == length // 2, 0, mode)
    wave = 2.0 * np.pi / length * mode
    sines, cosines = np.sin(angle), np.cos(angle)
    first_term = (sines * wave[None, :]) @ cosines.T
    second_term = (cosines * wave[None, :]) @ sines.T
    return ((second_term - first_term) / length).astype(np.float32)


def greet(partners):
    barrier = pltpu.get_barrier_semaphore()
    for partner in partners:
        pl.semaphore_signal(barrier, inc=1, device_id=partner, device_id_type=MESH)
    pl.semaphore_wait(barrier, len(partners))


def potential_kernel(
    bands,
    grids,
    pairs_ref,
    orb_hbm,
    core_hbm,
    tx_ref,
    ty_ref,
    tz_ref,
    out_ref,
    orb,
    core,
    part,
    x_in,
    z_out,
    z_in,
    own,
    line,
    gx,
    hx,
    sx,
    gy,
    hy,
    sy,
    dx,
    dz,
    other,
    fields,
    outgoing,
    orb_sem,
    core_sem,
    x_send,
    x_recv,
    z_send,
    z_recv,
    xp_send,
    xp_recv,
    xf_send,
    xf_recv,
    xb_send,
    xb_recv,
    yf_send,
    yf_recv,
    yb_send,
    yb_recv,
    in_send,
    in_recv,
    gy_send,
    gy_recv,
    out_send,
    out_recv,
):
    count, rows, y_cells, z_cells = orb.shape
    block = core.shape[1]
    slow = bands // FAST
    steps = out_send.shape[0]
    r_part = rows // bands
    chunk = r_part // steps
    piece_rows = rows // xp_send.shape[0]
    pieces = rows // piece_rows
    per_piece = piece_rows // chunk
    chunks = rows // chunk
    y_part = block // grids
    half = bands // 2
    xc_rows = math.gcd(XC_ROWS, chunk)
    me = lax.axis_index("band")
    slab = lax.axis_index("grid")
    spin = lax.axis_index("spin")
    my_slow, my_fast = lax.div(me, FAST), lax.rem(me, FAST)
    partner = {"band": my_slow * FAST + (1 - my_fast)}
    others = [{"band": lax.rem(my_slow + k, slow) * FAST + my_fast} for k in range(1, slow)]
    twin = {"spin": 1 - spin}
    my_block = pl.ds(pl.multiple_of(me * block, TILE), block)
    my_slab = pl.ds(pl.multiple_of(slab * rows, TILE), rows)
    mine = pl.ds(spin * half, half)
    theirs = pl.ds((1 - spin) * half, half)

    def remote(src, dst, send, recv, device):
        return pltpu.make_async_remote_copy(
            src_ref=src,
            dst_ref=dst,
            send_sem=send,
            recv_sem=recv,
            device_id=device,
            device_id_type=MESH,
        )

    def orb_copy(u):
        span = pl.ds(u * piece_rows, piece_rows)
        return pltpu.make_async_copy(orb_hbm.at[0, :, span], orb.at[:, span], orb_sem.at[u])

    def core_copy():
        return pltpu.make_async_copy(core_hbm.at[:, my_block], core, core_sem)

    def x_copy(c):
        span = pl.ds(c * chunk, chunk)
        return remote(
            part.at[1 - my_fast, span], x_in.at[span], x_send.at[c], x_recv.at[c], partner
        )

    def z_copy(c, k):
        span = pl.ds(c * chunk, chunk)
        return remote(
            z_out.at[lax.rem(my_slow + k, slow), span],
            z_in.at[k - 1, span],
            z_send.at[k - 1, c],
            z_recv.at[k - 1, c],
            others[k - 1],
        )

    def x_piece(u, k):
        q = lax.rem(slab + k, grids)
        start = pl.multiple_of(u * piece_rows, TILE)
        there = pl.multiple_of(slab * rows + u * piece_rows, TILE)
        return remote(
            line.at[0, pl.ds(q * y_part, y_part), pl.ds(start, piece_rows)],
            gx.at[0, :, pl.ds(there, piece_rows)],
            xp_send.at[u, k - 1],
            xp_recv.at[u, k - 1],
            {"grid": q},
        )

    def x_whole(k):
        q = lax.rem(slab + k, grids)
        return remote(
            line.at[1, pl.ds(q * y_part, y_part)],
            gx.at[1, :, my_slab],
            xf_send.at[k - 1],
            xf_recv.at[k - 1],
            {"grid": q},
        )

    def x_back(t, k):
        q = lax.rem(slab + k, grids)
        return remote(
            hx.at[t, :, pl.ds(pl.multiple_of(q * rows, TILE), rows)],
            sx.at[t, pl.ds(slab * y_part, y_part)],
            xb_send.at[t, k - 1],
            xb_recv.at[t, k - 1],
            {"grid": q},
        )

    def y_forward(t, s, k):
        q = lax.rem(me + k, bands)
        source = own if t == 0 else fields.at[2]
        return remote(
            source.at[q, pl.ds(s * chunk, chunk)],
            gy.at[t, pl.ds(s * chunk, chunk), my_block],
            yf_send.at[t, s, k - 1],
            yf_recv.at[t, s, k - 1],
            {"band": q},
        )

    def y_back(t, s, k):
        q = lax.rem(me + k, bands)
        return remote(
            hy.at[t, pl.ds(s * chunk, chunk), pl.ds(pl.multiple_of(q * block, TILE), block)],
            sy.at[t, me, pl.ds(s * chunk, chunk)],
            yb_send.at[t, s, k - 1],
            yb_recv.at[t, s, k - 1],
            {"band": q},
        )

    incoming = [own, dz, dx]

    def swap_in(f):
        return remote(incoming[f].at[theirs], other.at[f], in_send.at[f], in_recv.at[f], twin)

    def swap_steep(s):
        span = pl.ds(s * chunk, chunk)
        return remote(
            sy.at[0, theirs, span], other.at[3, :, span], gy_send.at[s], gy_recv.at[s], twin
        )

    def swap_out(s):
        span = pl.ds(s * chunk, chunk)
        return remote(
            outgoing.at[:, :, span],
            fields.at[:, mine, span],
            out_send.at[s],
            out_recv.at[s],
            twin,
        )

    def times(table, field):
        return jnp.dot(table, field, precision=EXACT, preferred_element_type=jnp.float32)

    def turned(value):
        return jnp.transpose(value, (1, 0, 2))

    def whole(value):
        return value.reshape(rows, block, z_cells)

    def split(value):
        return value.reshape(bands, r_part, block, z_cells)

    def along_third(field):
        return times(field.reshape(rows * block, z_cells), tz_ref[...]).reshape(field.shape)

    def along_first(t):
        for y in range(y_part):
            hx[t, y] = times(tx_ref[...], gx[t, y])
        for k in range(1, grids):
            x_back(t, k).start()
        sx[t, pl.ds(slab * y_part, y_part)] = hx[t, :, my_slab]

    def along_second(t, s):
        for k in range(1, bands):
            y_forward(t, s, k).wait_recv()
        for r in range(s * chunk, (s + 1) * chunk):
            hy[t, r] = times(ty_ref[...], gy[t, r])
        for k in range(1, bands):
            y_back(t, s, k).start()
        span = pl.ds(s * chunk, chunk)
        sy[t, me, span] = hy[t, span, my_block]

    def end_first(t):
        for k in range(1, grids):
            x_back(t, k).wait_recv()
        return split(turned(sx[t]))

    def end_second(t, s):
        for k in range(1, bands):
            y_back(t, s, k).wait_recv()

    def each(number, body):
        lax.fori_loop(0, number, lambda i, carry: (body(i), carry)[1], 0)

    each(pieces, lambda u: orb_copy(u).start())
    core_copy().start()
    greet(
        [twin]
        + [{"grid": lax.rem(slab + k, grids)} for k in range(1, grids)]
        + [{"band": lax.rem(me + k, bands)} for k in range(1, bands)]
    )
    first = pairs_ref[0, 0]
    last = first + pairs_ref[0, 1]
    weights = []
    for n in range(count):
        ident = me * count + n
        weights.append(jnp.where((ident >= first) & (ident < last), 0.5, 1.0).astype(jnp.float32))

    def squares(u):
        orb_copy(u).wait()

        def one_chunk(i):
            c = u * per_piece + i
            for r in range(chunk):
                row = c * chunk + r
                for b in range(bands):
                    total = jnp.zeros((block, z_cells), jnp.float32)
                    for n in range(count):
                        values = orb[n, row, b * block : (b + 1) * block].astype(jnp.float32)
                        total += weights[n] * (values * values)
                    part[b % FAST, row, b // FAST] = total
            x_copy(c).start()

        each(per_piece, one_chunk)

    def forward(u):
        def one_chunk(i):
            c = u * per_piece + i
            x_copy(c).wait_recv()
            span = pl.ds(c * chunk, chunk)
            for d in range(slow):
                z_out[d, span] = part[my_fast, span, d] + x_in[span, d]
            for k in range(1, slow):
                z_copy(c, k).start()

        each(per_piece, one_chunk)

    def collect(u):
        def one_chunk(i):
            c = u * per_piece + i
            span = pl.ds(c * chunk, chunk)
            total = 0.5 * core[span] + z_out[my_slow, span]
            for k in range(1, slow):
                z_copy(c, k).wait_recv()
                total += z_in[k - 1, span]
            j, s = lax.div(c, steps), lax.rem(c, steps)
            own[j, pl.ds(s * chunk, chunk)] = total

            @pl.when(j != me)
            def _():
                y_forward(0, s, lax.rem(j - me + bands, bands)).start()

            @pl.when(j == me)
            def _():
                gy[0, pl.ds(s * chunk, chunk), my_block] = total

        each(per_piece, one_chunk)
        group = piece_rows // r_part
        rows_here = own[pl.ds(u * group, group)].reshape(piece_rows, block, z_cells)
        start = pl.multiple_of(u * piece_rows, TILE)
        there = pl.multiple_of(slab * rows + u * piece_rows, TILE)
        line[0, :, pl.ds(start, piece_rows)] = turned(rows_here)
        for k in range(1, grids):
            x_piece(u, k).start()
        gx[0, :, pl.ds(there, piece_rows)] = line[
            0, pl.ds(slab * y_part, y_part), pl.ds(start, piece_rows)
        ]

    squares(0)
    squares(1)
    core_copy().wait()

    def sum_step(u):
        forward(u)

        @pl.when(u + 2 < pieces)
        def _():
            squares(u + 2)

        @pl.when(u >= 1)
        def _():
            collect(u - 1)

    each(pieces, sum_step)
    collect(pieces - 1)

    swap_in(0).start()
    dz[...] = along_third(own[...])
    swap_in(1).start()
    along_second(0, 0)
    for u in range(pieces):
        for k in range(1, grids):
            x_piece(u, k).wait_recv()
    along_first(0)
    for s in range(1, steps):
        along_second(0, s)
    dx[...] = end_first(0)
    swap_in(2).start()
    for f in range(3):
        swap_in(f).wait()

    def potential_rows(j, row):
        span = pl.ds(row, xc_rows)
        here = (spin * half + j, span)
        there = (j, span)
        n_own, n_other = own[here], other[(0,) + there]
        g_own = [dx[here], sy[(0,) + here], dz[here]]
        g_other = [other[(2,) + there], other[(3,) + there], other[(1,) + there]]
        s_own = g_own[0] * g_own[0] + g_own[1] * g_own[1] + g_own[2] * g_own[2]
        s_mix = g_own[0] * g_other[0] + g_own[1] * g_other[1] + g_own[2] * g_other[2]
        s_other = g_other[0] * g_other[0] + g_other[1] * g_other[1] + g_other[2] * g_other[2]
        energy, pull = jax.vjp(xc_energy, n_own, n_other, s_own, s_mix, s_other)
        derivs = pull(jnp.ones_like(energy))
        fields[(0,) + here] = derivs[0]
        outgoing[(0,) + there] = derivs[1]
        for a in range(3):
            fields[(1 + a,) + here] = 2.0 * derivs[2] * g_own[a] + derivs[3] * g_other[a]
            outgoing[(1 + a,) + there] = 2.0 * derivs[4] * g_other[a] + derivs[3] * g_own[a]

    def flux_out(s):
        swap_out(s).wait_recv()
        for k in range(1, bands):
            y_forward(1, s, k).start()
        span = pl.ds(s * chunk, chunk)
        gy[1, span, my_block] = fields[2, me, span]

    end_second(0, 0)
    swap_steep(0).start()
    for s in range(steps):
        swap_steep(s).wait_recv()
        per_group = chunk // xc_rows
        each(
            half * per_group,
            lambda i: potential_rows(
                lax.div(i, per_group), s * chunk + lax.rem(i, per_group) * xc_rows
            ),
        )
        swap_out(s).start()
        if s + 1 < steps:
            end_second(0, s + 1)
            swap_steep(s + 1).start()
        flux_out(s)

    line[1] = turned(whole(fields[1]))
    for k in range(1, grids):
        x_whole(k).start()
    gx[1, :, my_slab] = line[1, pl.ds(slab * y_part, y_part)]
    for s in range(steps - 1):
        along_second(1, s)
    dz[...] = fields[0] - along_third(fields[3])
    for k in range(1, grids):
        x_whole(k).wait_recv()
    along_first(1)
    along_second(1, steps - 1)
    dz[...] = dz[...] - end_first(1)
    for s in range(steps):
        end_second(1, s)
    out_ref[...] = whole(dz[...] - sy[1])

    def drain(c):
        x_copy(c).wait_send()
        for k in range(1, slow):
            z_copy(c, k).wait_send()

    each(chunks, drain)
    for k in range(1, grids):
        for u in range(pieces):
            x_piece(u, k).wait_send()
        x_whole(k).wait_send()
        x_back(0, k).wait_send()
        x_back(1, k).wait_send()
    for t in range(2):
        for s in range(steps):
            for k in range(1, bands):
                y_forward(t, s, k).wait_send()
                y_back(t, s, k).wait_send()
    for s in range(steps):
        swap_steep(s).wait_send()
        swap_out(s).wait_send()


def potential_call(orbitals, partial_bands, core_density, tables):
    bands, grids = lax.axis_size("band"), lax.axis_size("grid")
    _, count, rows, y_cells, z_cells = orbitals.shape
    block, slow = y_cells // bands, bands // FAST
    y_part, r_part = block // grids, rows // bands
    x_cells = rows * grids
    steps = r_part // math.gcd(CHUNK, r_part)
    chunks = bands * steps
    pieces = rows // max(r_part, TILE)
    half = bands // 2
    vmem = pl.BlockSpec(memory_space=pltpu.VMEM)
    hbm = pl.BlockSpec(memory_space=pl.ANY)
    dma = pltpu.SemaphoreType.DMA
    real = jnp.float32
    cells = (bands, r_part, block, z_cells)
    return pl.pallas_call(
        functools.partial(potential_kernel, bands, grids),
        out_shape=jax.ShapeDtypeStruct((rows, block, z_cells), real),
        in_specs=[pl.BlockSpec(memory_space=pltpu.SMEM), hbm, hbm] + [vmem] * 3,
        out_specs=vmem,
        scratch_shapes=[
            pltpu.VMEM((count, rows, y_cells, z_cells), jnp.bfloat16),
            pltpu.VMEM((rows, block, z_cells), real),
            pltpu.VMEM((FAST, rows, slow, block, z_cells), real),
            pltpu.VMEM((rows, slow, block, z_cells), real),
            pltpu.VMEM((slow, rows, block, z_cells), real),
            pltpu.VMEM((slow - 1, rows, block, z_cells), real),
            pltpu.VMEM(cells, real),
            pltpu.VMEM((2, block, rows, z_cells), real),
            pltpu.VMEM((2, y_part, x_cells, z_cells), real),
            pltpu.VMEM((2, y_part, x_cells, z_cells), real),
            pltpu.VMEM((2, block, rows, z_cells), real),
            pltpu.VMEM((2, r_part, y_cells, z_cells), real),
            pltpu.VMEM((2, r_part, y_cells, z_cells), real),
            pltpu.VMEM((2,) + cells, real),
            pltpu.VMEM(cells, real),
            pltpu.VMEM(cells, real),
            pltpu.VMEM((4, half) + cells[1:], real),
            pltpu.VMEM((4,) + cells, real),
            pltpu.VMEM((4, half) + cells[1:], real),
            dma((pieces,)),
            dma,
            dma((chunks,)),
            dma((chunks,)),
            dma((slow - 1, chunks)),
            dma((slow - 1, chunks)),
        ]
        + [dma((pieces, grids - 1))] * 2
        + [dma((grids - 1,))] * 2
        + [dma((2, grids - 1))] * 2
        + [dma((2, steps, bands - 1))] * 4
        + [dma((3,))] * 2
        + [dma((steps,))] * 4,
        compiler_params=pltpu.CompilerParams(
            collective_id=0, has_side_effects=True, vmem_limit_bytes=60 * 2**20
        ),
        name="potential",
    )(partial_bands, orbitals, core_density, *tables)


def per_device(orbitals, partial_bands, core_density):
    x_rows, y_cols, z_cells = core_density.shape
    tables = (
        jnp.asarray(spectral_table(x_rows * lax.axis_size("grid"))),
        jnp.asarray(spectral_table(y_cols)),
        jnp.asarray(spectral_table(z_cells).T),
    )
    return potential_call(orbitals, partial_bands, core_density, tables)[None]


def solution(mesh):
    in_specs = (P("spin", "band", "grid", None, None), P("spin", None), P("grid", None, None))
    out_specs = P("spin", "grid", "band", None)
    return jax.shard_map(
        per_device, mesh=mesh, in_specs=in_specs, out_specs=out_specs, check_vma=False
    )
```

time: 204 us -> 128 us (0.63)
  waiting for transfers between devices: 66.7 us -> 0 us
  Pallas kernels: 59.5 us -> 126 us
  starting transfers between devices: 27.9 us -> 0 us
  matrix products: 15.9 us -> 0 us
  other arithmetic: 11.4 us -> 0 us
  local copies, waits for them, and re-layouts: 12 us -> 1.87 us
  blocking collectives: 9.3 us -> 0 us
    pallas_call x1, Pallas kernels: 59.5 us -> 126 us  [potential_call(): pl.pallas_call(functools.partial(potential_kernel, bands, grids), out_sha...]
    all_to_all x7 -> x0, waiting for transfers between devices: 62.2 us -> none  [the longest x2 23.8 us: pencil_axes(): lax.all_to_all(second, 'band', split_axis=1, concat_axis=2, tiled=True)]
    all_to_all x7 -> x0, starting transfers between devices: 27.9 us -> none  [the longest x2 9.07 us: pencil_axes(): lax.all_to_all(along_second(lax.all_to_all(second, 'band', split_axis=1,...]
    dot_general x6 -> x0, matrix products: 15.9 us -> none  [the longest x2 11.9 us: along_third(): return jnp.einsum('fxyl,jl->fxyj', stack, table, precision=EXACT)]
    all_to_all x1 -> x0, blocking collectives: 9.3 us -> none  [pencil_axes(): lax.all_to_all(first, 'grid', split_axis=2, concat_axis=1, tiled=True)]
    mul x2 -> x0, other arithmetic: 5.04 us -> none  [the longest x1 5.01 us: per_device(): flux = 2.0 * ds_own[None] * steep + derivs[3][None] * other_steep]
    ppermute x1 -> x0, waiting for transfers between devices: 4.5 us -> none  [swapped(): return lax.ppermute(block, axis, route)]
    transpose x4 -> x0, local copies, waits for them, and re-layouts: 3.99 us -> none  [the longest x2 2 us: along_first(): return jnp.einsum('jl,flyz->fjyz', table, stack, precision=EXACT)]
  transfers between devices with their start and end apart: 8 -> 0, of which waited for: 8 -> 0; matrix products, arithmetic and copies ran while one was open for 6% -> 0% of each run, Pallas kernels for 0% -> 0%
where the time goes in v3:
time: 128 us
  Pallas kernels  126 us (98%)
  local copies, waits for them, and re-layouts  1.87 us (1%)
    pallas_call x1, Pallas kernels, potential_call(): pl.pallas_call(functools.partial(potential_kernel, bands, grids), out_sha...  126 us

profile of v3, /device:TPU:0, one launch (start us, length us, event | category | flops | bytes accessed | tf_op | source)
XLA Modules:
  0.0 127.6 jit_solution(719482476659331992)
XLA Ops:
  0.0 125.8 %potential.1 = f32[64,16,128]{2,1,0:T(8,128)} custom-call(s32[1,2]{1,0:T(1,128)} %pairs_ref.1, bf16[1,8,64,128,128]{4,3,2,1,0:T(8,128)(2,1)} %orb_hbm.1, f32[64,128,128]{2,1,0:T(8,128)} %core_hbm.1, f32[128,128]{1,0:T(8,128)} %constant.4.clone.tx_ref.ty_ref, f32[128,128]{1,0:T(8,128)} %constant.4.clone.tx_ref.ty_ref, f32[128,128]{1,0:T(8,128)} %constant.5.clone.tz_ref), custom_call_target="tpu_custom_call" | custom-call | tf_op jit(solution)/shard_map/potential/pallas_call | solution.py:532
  125.8 1.9 %copy.8 = f32[1,64,16,128]{3,2,1,0:T(8,128)} copy(f32[1,64,16,128]{3,2,1,0:T(8,128)} %bitcast.1) | data formatting | bytes 1048576

commit v4 on v3

--- a/solution.py
+++ b/solution.py
@@ -92,13 +92,6 @@
     return ((second_term - first_term) / length).astype(np.float32)
 
 
-def greet(partners):
-    barrier = pltpu.get_barrier_semaphore()
-    for partner in partners:
-        pl.semaphore_signal(barrier, inc=1, device_id=partner, device_id_type=MESH)
-    pl.semaphore_wait(barrier, len(partners))
-
-
 def potential_kernel(
     bands,
     grids,
@@ -114,7 +107,9 @@
     part,
     x_in,
     z_out,
-    z_in,
+    p_in,
+    w_out,
+    w_in,
     own,
     line,
     gx,
@@ -132,8 +127,10 @@
     core_sem,
     x_send,
     x_recv,
-    z_send,
-    z_recv,
+    p_send,
+    p_recv,
+    w_send,
+    w_recv,
     xp_send,
     xp_recv,
     xf_send,
@@ -169,7 +166,10 @@
     spin = lax.axis_index("spin")
     my_slow, my_fast = lax.div(me, FAST), lax.rem(me, FAST)
     partner = {"band": my_slow * FAST + (1 - my_fast)}
-    others = [{"band": lax.rem(my_slow + k, slow) * FAST + my_fast} for k in range(1, slow)]
+    pairs = slow // 2
+    my_pair = lax.div(my_slow, 2)
+    my_kind = lax.rem(my_slow + my_pair, 2)
+    beside = {"band": (my_slow + 1 - 2 * lax.rem(my_slow, 2)) * FAST + my_fast}
     twin = {"spin": 1 - spin}
     my_block = pl.ds(pl.multiple_of(me * block, TILE), block)
     my_slab = pl.ds(pl.multiple_of(slab * rows, TILE), rows)
@@ -199,14 +199,25 @@
             part.at[1 - my_fast, span], x_in.at[span], x_send.at[c], x_recv.at[c], partner
         )
 
+    def pair_copy(c):
+        span = pl.ds(c * chunk, chunk)
+        return remote(
+            z_out.at[1 - my_kind, :, span],
+            p_in.at[:, span],
+            p_send.at[c],
+            p_recv.at[c],
+            beside,
+        )
+
     def z_copy(c, k):
         span = pl.ds(c * chunk, chunk)
-        return remote(
-            z_out.at[lax.rem(my_slow + k, slow), span],
-            z_in.at[k - 1, span],
-            z_send.at[k - 1, c],
-            z_recv.at[k - 1, c],
-            others[k - 1],
+        h = lax.rem(my_pair + k, pairs)
+        return remote(
+            w_out.at[h, span],
+            w_in.at[k - 1, span],
+            w_send.at[k - 1, c],
+            w_recv.at[k - 1, c],
+            {"band": (2 * h + lax.rem(my_kind + h, 2)) * FAST + my_fast},
         )
 
     def x_piece(u, k):
@@ -329,11 +340,14 @@
 
     each(pieces, lambda u: orb_copy(u).start())
     core_copy().start()
-    greet(
+    partners = (
         [twin]
         + [{"grid": lax.rem(slab + k, grids)} for k in range(1, grids)]
         + [{"band": lax.rem(me + k, bands)} for k in range(1, bands)]
     )
+    barrier = pltpu.get_barrier_semaphore()
+    for target in partners:
+        pl.semaphore_signal(barrier, inc=1, device_id=target, device_id_type=MESH)
     first = pairs_ref[0, 0]
     last = first + pairs_ref[0, 1]
     weights = []
@@ -354,9 +368,11 @@
                         values = orb[n, row, b * block : (b + 1) * block].astype(jnp.float32)
                         total += weights[n] * (values * values)
                     part[b % FAST, row, b // FAST] = total
-            x_copy(c).start()
 
         each(per_piece, one_chunk)
+
+    def send_squares(u):
+        each(per_piece, lambda i: x_copy(u * per_piece + i).start())
 
     def forward(u):
         def one_chunk(i):
@@ -364,8 +380,18 @@
             x_copy(c).wait_recv()
             span = pl.ds(c * chunk, chunk)
             for d in range(slow):
-                z_out[d, span] = part[my_fast, span, d] + x_in[span, d]
-            for k in range(1, slow):
+                z_out[(d + d // 2) % 2, d // 2, span] = part[my_fast, span, d] + x_in[span, d]
+            pair_copy(c).start()
+
+        each(per_piece, one_chunk)
+
+    def join(u):
+        def one_chunk(i):
+            c = u * per_piece + i
+            pair_copy(c).wait_recv()
+            span = pl.ds(c * chunk, chunk)
+            w_out[:, span] = z_out[my_kind, :, span] + p_in[:, span]
+            for k in range(1, pairs):
                 z_copy(c, k).start()
 
         each(per_piece, one_chunk)
@@ -374,10 +400,10 @@
         def one_chunk(i):
             c = u * per_piece + i
             span = pl.ds(c * chunk, chunk)
-            total = 0.5 * core[span] + z_out[my_slow, span]
-            for k in range(1, slow):
+            total = 0.5 * core[span] + w_out[my_pair, span]
+            for k in range(1, pairs):
                 z_copy(c, k).wait_recv()
-                total += z_in[k - 1, span]
+                total += w_in[k - 1, span]
             j, s = lax.div(c, steps), lax.rem(c, steps)
             own[j, pl.ds(s * chunk, chunk)] = total
 
@@ -403,6 +429,9 @@
 
     squares(0)
     squares(1)
+    pl.semaphore_wait(barrier, len(partners))
+    send_squares(0)
+    send_squares(1)
     core_copy().wait()
 
     def sum_step(u):
@@ -411,12 +440,19 @@
         @pl.when(u + 2 < pieces)
         def _():
             squares(u + 2)
+            send_squares(u + 2)
 
         @pl.when(u >= 1)
         def _():
-            collect(u - 1)
+            join(u - 1)
+
+        @pl.when(u >= 2)
+        def _():
+            collect(u - 2)
 
     each(pieces, sum_step)
+    join(pieces - 1)
+    collect(pieces - 2)
     collect(pieces - 1)
 
     swap_in(0).start()
@@ -494,7 +530,8 @@
 
     def drain(c):
         x_copy(c).wait_send()
-        for k in range(1, slow):
+        pair_copy(c).wait_send()
+        for k in range(1, pairs):
             z_copy(c, k).wait_send()
 
     each(chunks, drain)
@@ -539,8 +576,10 @@
             pltpu.VMEM((rows, block, z_cells), real),
             pltpu.VMEM((FAST, rows, slow, block, z_cells), real),
             pltpu.VMEM((rows, slow, block, z_cells), real),
-            pltpu.VMEM((slow, rows, block, z_cells), real),
-            pltpu.VMEM((slow - 1, rows, block, z_cells), real),
+            pltpu.VMEM((2, slow // 2, rows, block, z_cells), real),
+            pltpu.VMEM((slow // 2, rows, block, z_cells), real),
+            pltpu.VMEM((slow // 2, rows, block, z_cells), real),
+            pltpu.VMEM((slow // 2 - 1, rows, block, z_cells), real),
             pltpu.VMEM(cells, real),
             pltpu.VMEM((2, block, rows, z_cells), real),
             pltpu.VMEM((2, y_part, x_cells, z_cells), real),
@@ -558,8 +597,10 @@
             dma,
             dma((chunks,)),
             dma((chunks,)),
-            dma((slow - 1, chunks)),
-            dma((slow - 1, chunks)),
+            dma((chunks,)),
+            dma((chunks,)),
+            dma((slow // 2 - 1, chunks)),
+            dma((slow // 2 - 1, chunks)),
         ]
         + [dma((pieces, grids - 1))] * 2
         + [dma((grids - 1,))] * 2

time: 128 us -> 123 us (0.961)
  Pallas kernels: 126 us -> 121 us
    pallas_call x1, Pallas kernels: 126 us -> 121 us  [potential_call(): pl.pallas_call(functools.partial(potential_kernel, bands, grids), out_sha...]
where the time goes in v4:
time: 123 us; the launch traced here: 122 us
  Pallas kernels  121 us (98%)
  local copies, waits for them, and re-layouts  1.87 us (2%)
    pallas_call x1, Pallas kernels, potential_call(): pl.pallas_call(functools.partial(potential_kernel, bands, grids), out_sha...  121 us

profile of v4, /device:TPU:0, one launch (start us, length us, event | category | flops | bytes accessed | tf_op | source)
XLA Modules:
  0.0 122.5 jit_solution(5593217802549266407)
XLA Ops:
  0.0 120.6 %potential.1 = f32[64,16,128]{2,1,0:T(8,128)} custom-call(s32[1,2]{1,0:T(1,128)} %pairs_ref.1, bf16[1,8,64,128,128]{4,3,2,1,0:T(8,128)(2,1)} %orb_hbm.1, f32[64,128,128]{2,1,0:T(8,128)} %core_hbm.1, f32[128,128]{1,0:T(8,128)} %constant.4.clone.tx_ref.ty_ref, f32[128,128]{1,0:T(8,128)} %constant.4.clone.tx_ref.ty_ref, f32[128,128]{1,0:T(8,128)} %constant.5.clone.tz_ref), custom_call_target="tpu_custom_call" | custom-call | tf_op jit(solution)/shard_map/potential/pallas_call | solution.py:569
  120.6 1.9 %copy.8 = f32[1,64,16,128]{3,2,1,0:T(8,128)} copy(f32[1,64,16,128]{3,2,1,0:T(8,128)} %bitcast.1) | data formatting | bytes 1048576

commit v5 on v4

--- a/solution.py
+++ b/solution.py
@@ -338,7 +338,14 @@
     def each(number, body):
         lax.fori_loop(0, number, lambda i, carry: (body(i), carry)[1], 0)
 
-    each(pieces, lambda u: orb_copy(u).start())
+    def order(u):
+        if pieces != bands:
+            return u
+        v, fast = u % slow, u // slow
+        late = v // pairs
+        return (v + late * (pairs + slow - 1 - 2 * v)) * FAST + fast
+
+    each(pieces, lambda u: orb_copy(order(u)).start())
     core_copy().start()
     partners = (
         [twin]
@@ -427,33 +434,33 @@
             0, pl.ds(slab * y_part, y_part), pl.ds(start, piece_rows)
         ]
 
-    squares(0)
-    squares(1)
+    squares(order(0))
+    squares(order(1))
     pl.semaphore_wait(barrier, len(partners))
-    send_squares(0)
-    send_squares(1)
+    send_squares(order(0))
+    send_squares(order(1))
     core_copy().wait()
 
     def sum_step(u):
-        forward(u)
+        forward(order(u))
 
         @pl.when(u + 2 < pieces)
         def _():
-            squares(u + 2)
-            send_squares(u + 2)
+            squares(order(u + 2))
+            send_squares(order(u + 2))
 
         @pl.when(u >= 1)
         def _():
-            join(u - 1)
+            join(order(u - 1))
 
         @pl.when(u >= 2)
         def _():
-            collect(u - 2)
+            collect(order(u - 2))
 
     each(pieces, sum_step)
-    join(pieces - 1)
-    collect(pieces - 2)
-    collect(pieces - 1)
+    join(order(pieces - 1))
+    collect(order(pieces - 2))
+    collect(order(pieces - 1))
 
     swap_in(0).start()
     dz[...] = along_third(own[...])

time: 123 us -> 115 us (0.935)
  Pallas kernels: 121 us -> 113 us
    pallas_call x1, Pallas kernels: 121 us -> 113 us  [potential_call(): pl.pallas_call(functools.partial(potential_kernel, bands, grids), out_sha...]
where the time goes in v5:
time: 115 us
  Pallas kernels  113 us (98%)
  local copies, waits for them, and re-layouts  1.87 us (2%)
    pallas_call x1, Pallas kernels, potential_call(): pl.pallas_call(functools.partial(potential_kernel, bands, grids), out_sha...  113 us

profile of v5, /device:TPU:0, one launch (start us, length us, event | category | flops | bytes accessed | tf_op | source)
XLA Modules:
  0.0 114.6 jit_solution(1594545357200207076)
XLA Ops:
  0.0 112.7 %potential.1 = f32[64,16,128]{2,1,0:T(8,128)} custom-call(s32[1,2]{1,0:T(1,128)} %pairs_ref.1, bf16[1,8,64,128,128]{4,3,2,1,0:T(8,128)(2,1)} %orb_hbm.1, f32[64,128,128]{2,1,0:T(8,128)} %core_hbm.1, f32[128,128]{1,0:T(8,128)} %constant.4.clone.tx_ref.ty_ref, f32[128,128]{1,0:T(8,128)} %constant.4.clone.tx_ref.ty_ref, f32[128,128]{1,0:T(8,128)} %constant.5.clone.tz_ref), custom_call_target="tpu_custom_call" | custom-call | tf_op jit(solution)/shard_map/potential/pallas_call | solution.py:576
  112.7 1.9 %copy.8 = f32[1,64,16,128]{3,2,1,0:T(8,128)} copy(f32[1,64,16,128]{3,2,1,0:T(8,128)} %bitcast.1) | data formatting | bytes 1048576
